TPU v7x, 32 devices: a whole 2x2x4 slice. The times are simulated.
32 devices in a mesh: gx: 4 (over y, x), gy: 8 (over z, core).
Axes of the slice: x: 2, y: 2, z: 4, core: 2. Of those that a mesh axis runs over, the one named last changes fastest.
Arguments:
- fine_nodes: bfloat16 [65536, 256], P(('gx', 'gy')), may hold values from -6 to 6
- fine_weights: bfloat16 [6, 256, 256], replicated, may hold values from -0.375 to 0.375
- coarse_weights: bfloat16 [6, 256, 256], replicated, may hold values from -0.375 to 0.375
- top_weights: bfloat16 [6, 256, 256], replicated, may hold values from -0.375 to 0.375
- gains: float32 [3, 256], replicated, may hold values from 0.1 to 1.9
- send_list: int32 [4, 8, 4, 512], P('gx', 'gy'), may hold values from 0 to 2047
- fine_sender: int32 [4, 8, 8192], P('gx', 'gy'), may hold values from 0 to 4095, as said below
- fine_receiver: int32 [4, 8, 8192], P('gx', 'gy'), may hold values from 0 to 2048, as said below
- pool_owner: int32 [65536, 1], P(('gx', 'gy')), may hold values from 0 to 3; in each aligned block of 2048 rows (0 to 2047, 2048 to 4095, ...) at most 1024 rows name the same one
- pool_local: int32 [65536], P(('gx', 'gy')), may hold values from 0 to 255
- coarse_sender: int32 [8, 4096], P('gy', 'gx'), may hold values from 0 to 1023
- coarse_receiver: int32 [8, 4096], P('gy', 'gx'), may hold values from 0 to 255
- top_parent: int32 [8, 1024], P('gy', 'gx'), may hold values from 0 to 127
- top_sender: int32 [8, 512], P('gy'), may hold values from 0 to 127
- top_receiver: int32 [8, 512], P('gy'), may hold values from 0 to 127
Outputs:
- fine_state: bfloat16 [65536, 256], P(('gx', 'gy'))
- coarse_state: bfloat16 [8, 1024, 256], P('gy', 'gx')
Inputs may be any that keep to these rules, and one draw needn't show every extreme that they name: `fine_sender`: values below 2048 name the device's own nodes; larger values name a halo row of a neighbour that exists. `fine_receiver`: 2048 marks an empty slot; a device's live slots come first, and some device has no empty slot. `pool_owner`: among the rows of one device no member is named more than 1024 times.
All inputs are finite; a program needn't handle non-finite values.
Results may differ from a plain program's by a relative error of at most 0.015.
Values may be sent and summed in bfloat16 or wider, within the bound.
No kernel may reach another device: no remote copies, remote signals or barrier semaphores. Data moves between devices by JAX's collectives and lax.ppermute only.
A program may use at most 64 MiB of HBM per device.

v0:
```python
import math

import jax
import jax.numpy as jnp
from jax import lax
from jax.sharding import PartitionSpec as P


def passed_along(block, axis, distance):
    devices = range(lax.axis_size(axis))
    route = [(i - distance, i) for i in devices if i - distance in devices]
    return lax.ppermute(block, axis, route)


def project(states, weights):
    sender_term = jnp.dot(states, weights[0], preferred_element_type=jnp.float32).astype(
        jnp.bfloat16
    )
    receiver_term = jnp.dot(states, weights[1], preferred_element_type=jnp.float32).astype(
        jnp.bfloat16
    )
    return (sender_term, receiver_term)


def gather_messages(fetch, receiver_term, receivers, weight_out, count, most):
    edges = receivers.shape[0]
    block = math.gcd(edges, most)
    width = receiver_term.shape[1]

    def advance(summed, turn):
        begin = turn * block
        targets = lax.dynamic_slice_in_dim(receivers, begin, block)
        before = fetch(begin, block) + jnp.take(
            receiver_term, jnp.minimum(targets, count - 1), axis=0
        ).astype(jnp.float32)
        hidden = jax.nn.silu(before).astype(jnp.bfloat16)
        message = jnp.dot(hidden, weight_out, preferred_element_type=jnp.float32)
        return (summed.at[targets].add(message, mode="drop"), None)

    turns = jnp.arange(edges // block, dtype=jnp.int32)
    summed, unused = lax.scan(advance, jnp.zeros((count, width), jnp.float32), turns)
    return summed


def update_nodes(states, aggregate, weights, gain):
    merged = jnp.dot(states, weights[3], preferred_element_type=jnp.float32)
    merged = merged + jnp.dot(
        aggregate.astype(jnp.bfloat16), weights[4], preferred_element_type=jnp.float32
    )
    inner = jax.nn.silu(merged).astype(jnp.bfloat16)
    output = jnp.dot(inner, weights[5], preferred_element_type=jnp.float32)
    centred = output - jnp.mean(output, axis=1, keepdims=True)
    spread = jnp.mean(centred * centred, axis=1, keepdims=True)
    return (states.astype(jnp.float32) + gain * centred * lax.rsqrt(spread + 1e-05)).astype(
        jnp.bfloat16
    )


def table_fetch(table, senders):

    def fetch(begin, rows):
        picked = lax.dynamic_slice_in_dim(senders, begin, rows)
        return jnp.take(table, picked, axis=0).astype(jnp.float32)

    return fetch


def body(
    fine_nodes,
    fine_weights,
    coarse_weights,
    top_weights,
    gains,
    send_list,
    fine_sender,
    fine_receiver,
    pool_owner,
    pool_local,
    coarse_sender,
    coarse_receiver,
    top_parent,
    top_sender,
    top_receiver,
):
    nodes = fine_nodes.shape[0]
    width = fine_nodes.shape[1]
    members = lax.axis_size("gx")
    coarse_rows = nodes // 8
    top_rows = coarse_rows * members // 8
    lists = send_list.reshape(4, -1)
    fine_send, fine_recv = project(fine_nodes, fine_weights)
    pieces = [fine_send]
    for slot, offset in ((0, 1), (1, -1)):
        pieces.append(passed_along(jnp.take(fine_send, lists[slot], axis=0), "gx", offset))
    for slot, offset in ((2, 1), (3, -1)):
        pieces.append(passed_along(jnp.take(fine_send, lists[slot], axis=0), "gy", offset))
    table = jnp.concatenate(pieces, axis=0)
    fine_aggregate = gather_messages(
        table_fetch(table, fine_sender.reshape(-1)),
        fine_recv,
        fine_receiver.reshape(-1),
        fine_weights[2],
        nodes,
        4096,
    )
    fine_one = update_nodes(fine_nodes, fine_aggregate, fine_weights, gains[0])
    owner = pool_owner.reshape(-1)
    parent = owner * coarse_rows + pool_local
    partial_value = (
        jnp.zeros((members * coarse_rows, width), jnp.float32)
        .at[parent]
        .add(fine_one.astype(jnp.float32))
    )
    partial_count = jnp.zeros((members * coarse_rows,), jnp.float32).at[parent].add(1.0)
    coarse_sum, child_count = (
        lax.psum_scatter(
            partial_value.astype(jnp.bfloat16), "gx", scatter_dimension=0, tiled=True
        ).astype(jnp.float32),
        lax.psum_scatter(
            partial_count.astype(jnp.bfloat16), "gx", scatter_dimension=0, tiled=True
        ).astype(jnp.float32),
    )
    coarse_zero = (coarse_sum / jnp.maximum(child_count, 1.0)[:, None]).astype(jnp.bfloat16)
    coarse_send, coarse_recv = project(coarse_zero, coarse_weights)
    coarse_senders = coarse_sender.reshape(-1)
    piece = lax.all_gather(coarse_send, "gx", axis=0, tiled=True)
    inside = (coarse_senders >= 0) & (coarse_senders < piece.shape[0])
    picked = jnp.take(piece, jnp.clip(coarse_senders, 0, piece.shape[0] - 1), axis=0).astype(
        jnp.float32
    )
    gathered = jnp.where(inside[:, None], picked, 0.0)

    def slice_gathered(begin, rows):
        return gathered

    coarse_aggregate = gather_messages(
        slice_gathered,
        coarse_recv,
        coarse_receiver.reshape(-1),
        coarse_weights[2],
        coarse_rows,
        4096,
    )
    coarse_one = update_nodes(coarse_zero, coarse_aggregate, coarse_weights, gains[1])
    parents = top_parent.reshape(-1)
    partial_top = (
        jnp.zeros((top_rows, width), jnp.float32).at[parents].add(coarse_one.astype(jnp.float32))
    )
    partial_top_count = jnp.zeros((top_rows,), jnp.float32).at[parents].add(1.0)
    top_sum, top_count = (
        lax.psum(partial_top.astype(jnp.bfloat16), "gx").astype(jnp.float32),
        lax.psum(partial_top_count.astype(jnp.bfloat16), "gx").astype(jnp.float32),
    )
    top_zero = (top_sum / jnp.maximum(top_count, 1.0)[:, None]).astype(jnp.bfloat16)
    top_send, top_recv = project(top_zero, top_weights)
    top_aggregate = gather_messages(
        table_fetch(top_send, top_sender.reshape(-1)),
        top_recv,
        top_receiver.reshape(-1),
        top_weights[2],
        top_rows,
        4096,
    )
    top_one = update_nodes(top_zero, top_aggregate, top_weights, gains[2])
    coarse_two = (
        coarse_one.astype(jnp.float32) + jnp.take(top_one, parents, axis=0).astype(jnp.float32)
    ).astype(jnp.bfloat16)
    whole = lax.all_gather(coarse_two, "gx", axis=0, tiled=True)
    lifted = jnp.take(whole, parent, axis=0)
    fine_state = (fine_one.astype(jnp.float32) + lifted.astype(jnp.float32)).astype(jnp.bfloat16)
    return (fine_state, coarse_two[None])


def solution(mesh):
    placed = (
        P(("gx", "gy"), None),
        P(),
        P(),
        P(),
        P(),
        P("gx", "gy", None, None),
        P("gx", "gy", None),
        P("gx", "gy", None),
        P(("gx", "gy"), None),
        P(("gx", "gy")),
        P("gy", "gx"),
        P("gy", "gx"),
        P("gy", "gx"),
        P("gy", None),
        P("gy", None),
    )
    return jax.shard_map(
        body,
        mesh=mesh,
        in_specs=placed,
        out_specs=(P(("gx", "gy"), None), P("gy", "gx", None)),
        check_vma=False,
    )
```

profile of v0, /device:TPU:0, one launch (start us, length us, event | category | flops | bytes accessed | tf_op | source)
XLA Modules:
  0.0 395.7 jit_solution(5768898327504365994)
XLA Ops:
  12.6 5.6 %collective-permute-start = (bf16[512,256]{1,0:T(8,128)(2,1)}, bf16[512,256]{1,0:T(8,128)(2,1)}, u32[]{:S(2)}, u32[]{:S(2)}) collective-permute-start(bf16[512,256]{1,0:T(8,128)(2,1)} %broadcast_select_fusion.3), channel_id=1, source_target_pairs={{0,8},{8,16},{16,24},{1,9},{9,17},{17,25},{2,10},{10,18},{18,26},{... | collective-permute-start | bytes 786440 | tf_op jit(solution)/shard_map/ppermute | solution.py:12
  25.1 2.1 collective-permute-start.2
  34.7 2.7 fusion.46
  41.0 14.7 %scatter_custom_fusion.2 = f32[1024]{0:T(1024)S(1)} fusion(s32[2048]{0:T(1024)S(1)} %get-tuple-element.111, f32[2048]{0:T(1024)S(1)} %broadcast.313, f32[]{:T(128)} %constant.135.clone.1), kind=kCustom, calls=%fused_computation.167 | custom fusion | flops 2048 | bytes 4100 | tf_op jit(solution)/shard_map/scatter-add | solution.py:114
  55.7 2.3 scatter_custom_fusion.5
  59.2 11.6 %all-reduce.1 = (bf16[1024]{0:T(1024)(128)(2,1)}, bf16[128]{0:T(256)(128)(2,1)S(1)}) all-reduce(bf16[1024]{0:T(1024)(128)(2,1)S(1)} %convert_element_type.145, bf16[128]{0:T(256)(128)(2,1)S(1)} %convert_element_type.160), channel_id=3, replica_groups=mesh['gx'=4,'gy'=8] {'gx'}, use_global_device_ids=true, to_apply=%region_8.10.clone | all-reduce | flops 1152 | bytes 4608
  71.9 2.3 copy.34
  80.1 131.3 %while.2 = (s32[]{:T(128)}, f32[2048,256]{1,0:T(8,128)S(1)}, s32[2]{0:T(128)S(1)}, s32[8192]{0:T(1024)S(1)}, s32[8192]{0:T(1024)S(1)}, /*index=5*/bf16[4096,256]...) while((s32[]{:T(128)}, f32[2048,256]{1,0:T(8,128)S(1)}, ...), condition=%wide.region_2.4_spmd, body=%wide.region_0.3_spmd.sunk | while | flops 548507648 | bytes 30195924 | solution.py:41
  81.3 17.0 %gather_fusion = bf16[4096,256]{1,0:T(8,128)(2,1)} fusion(bf16[2048,256]{1,0:T(8,128)(2,1)S(1)} %get-tuple-element.235, s32[4096]{0:T(1024)S(1)} %get-tuple-element.201), kind=kCustom, calls=%fused_computation.2.clone.1 | custom fusion | bytes 4210688 | tf_op jit(solution)/shard_map/while/body/eval_jaxpr/jit(_take)/gather | solution.py:33
  98.3 17.7 %gather_fusion.1 = bf16[4096,256]{1,0:T(8,128)(2,1)} fusion(bf16[4096,256]{1,0:T(8,128)(2,1)} %get-tuple-element.234, s32[4096]{0:T(1024)S(1)} %get-tuple-element.202), kind=kCustom, calls=%fused_computation.1.clone.1 | custom fusion | bytes 4210688 | tf_op jit(solution)/shard_map/while/body/eval_jaxpr/jit(_take)/gather | solution.py:63
  116.0 6.1 %fusion.123 = f32[4096,256]{1,0:T(8,128)} fusion(bf16[256,256]{1,0:T(8,128)(2,1)S(1)} %copy-done.6, bf16[4096,256]{1,0:T(8,128)(2,1)} %gather_fusion, bf16[4096,256]{1,0:T(8,128)(2,1)} %gather_fusion.1, pred[4096]{0:T(1024)(128)(4,1)S(1)} %get-tuple-element.203, pred[4096]{0:T(1024)(128)(4,1)S(1)} %get-tuple-element.204), kind=kOutput, calls=%fused_computation.20.clone.1 | convolution fusion | flops 547356672 | bytes 8527872 | tf_op jit(solution)/shard_map/while/body/eval_jaxpr/dot_general | solution.py:37
  122.2 23.6 %scatter_fusion = f32[2048,256]{1,0:T(8,128)S(1)} fusion(f32[2048,256]{1,0:T(8,128)S(1)} %get-tuple-element.218, s32[4096]{0:T(1024)S(1)} %get-tuple-element.200, f32[4096,256]{1,0:T(8,128)} %fusion.123), kind=kCustom, calls=%fused_computation.12.clone.1 | custom fusion | flops 1048576 | bytes 12599296 | tf_op jit(solution)/shard_map/while/body/eval_jaxpr/scatter-add | solution.py:38
  147.0 17.0 %gather_fusion = bf16[4096,256]{1,0:T(8,128)(2,1)} fusion(bf16[2048,256]{1,0:T(8,128)(2,1)S(1)} %get-tuple-element.235, s32[4096]{0:T(1024)S(1)} %get-tuple-element.201), kind=kCustom, calls=%fused_computation.2.clone.1 | custom fusion | bytes 4210688 | tf_op jit(solution)/shard_map/while/body/eval_jaxpr/jit(_take)/gather | solution.py:33
  163.9 17.7 %gather_fusion.1 = bf16[4096,256]{1,0:T(8,128)(2,1)} fusion(bf16[4096,256]{1,0:T(8,128)(2,1)} %get-tuple-element.234, s32[4096]{0:T(1024)S(1)} %get-tuple-element.202), kind=kCustom, calls=%fused_computation.1.clone.1 | custom fusion | bytes 4210688 | tf_op jit(solution)/shard_map/while/body/eval_jaxpr/jit(_take)/gather | solution.py:63
  181.7 6.1 %fusion.123 = f32[4096,256]{1,0:T(8,128)} fusion(bf16[256,256]{1,0:T(8,128)(2,1)S(1)} %copy-done.6, bf16[4096,256]{1,0:T(8,128)(2,1)} %gather_fusion, bf16[4096,256]{1,0:T(8,128)(2,1)} %gather_fusion.1, pred[4096]{0:T(1024)(128)(4,1)S(1)} %get-tuple-element.203, pred[4096]{0:T(1024)(128)(4,1)S(1)} %get-tuple-element.204), kind=kOutput, calls=%fused_computation.20.clone.1 | convolution fusion | flops 547356672 | bytes 8527872 | tf_op jit(solution)/shard_map/while/body/eval_jaxpr/dot_general | solution.py:37
  187.8 23.6 %scatter_fusion = f32[2048,256]{1,0:T(8,128)S(1)} fusion(f32[2048,256]{1,0:T(8,128)S(1)} %get-tuple-element.218, s32[4096]{0:T(1024)S(1)} %get-tuple-element.200, f32[4096,256]{1,0:T(8,128)} %fusion.123), kind=kCustom, calls=%fused_computation.12.clone.1 | custom fusion | flops 1048576 | bytes 12599296 | tf_op jit(solution)/shard_map/while/body/eval_jaxpr/scatter-add | solution.py:38
  211.5 3.8 fusion.99
  221.1 13.0 %scatter_custom_fusion.1 = f32[1024,256]{1,0:T(8,128)} fusion(s32[2048]{0:T(1024)S(1)} %copy-done.11, f32[2048,256]{1,0:T(8,128)} %copy.35, f32[]{:T(128)} %constant.135.clone.1), kind=kCustom, calls=%fused_computation.52 | custom fusion | flops 524288 | bytes 1049088 | tf_op jit(solution)/shard_map/scatter-add | solution.py:112
  234.1 2.2 copy.36
  237.2 26.1 %reduce-scatter.2.cloned.1.call-done = bf16[256,256]{0,1:T(8,128)(2,1)} async-done(((bf16[1024,256]{0,1:T(8,128)(2,1)}), bf16[256,256]{0,1:T(8,128)(2,1)}) %reduce-scatter.2.cloned.1.call-update) | async-done | bytes 131088 | tf_op jit(solution)/shard_map/reduce_scatter | solution.py:116
  264.6 10.5 %all_gather.6 = bf16[1024,256]{1,0:T(8,128)(2,1)S(1)} all-gather(bf16[256,256]{1,0:T(8,128)(2,1)S(1)} %convolution_convert_fusion.3), channel_id=1, replica_groups=mesh['gx'=4,'gy'=8] {'gx'}, dimensions={0}, use_global_device_ids=true | all-gather | bytes 655360 | tf_op jit(solution)/shard_map/all_gather | solution.py:126
  275.1 3.9 gather_fusion.2
  280.2 5.0 %gather_fusion.3 = bf16[1024,256]{1,0:T(8,128)(2,1)} fusion(bf16[256,256]{1,0:T(8,128)(2,1)S(1)} %convolution_convert_fusion.2, s32[1024]{0:T(1024)S(1)} %get-tuple-element.140), kind=kCustom, calls=%fused_computation.9 | custom fusion | bytes 1052672 | tf_op jit(solution)/shard_map/while/body/eval_jaxpr/jit(_take)/gather | solution.py:33
  285.1 2.7 fusion.15
  287.8 6.6 %scatter_custom_fusion.3 = f32[256,256]{1,0:T(8,128)S(1)} fusion(s32[1024]{0:T(1024)S(1)} %bitcast.137, f32[1024,256]{1,0:T(8,128)} %fusion.15, f32[]{:T(128)} %constant.135.clone.1), kind=kCustom, calls=%fused_computation.112 | custom fusion | flops 262144 | bytes 262656 | tf_op jit(solution)/shard_map/while/body/eval_jaxpr/scatter-add | solution.py:38
  300.8 42.0 %all-reduce.4.cloned.1.call-done = bf16[128,256]{1,0:T(8,128)(2,1)} async-done(((bf16[128,256]{1,0:T(8,128)(2,1)}), bf16[128,256]{1,0:T(8,128)(2,1)}) %all-reduce.4.cloned.1.call-update) | async-done | bytes 65552 | tf_op jit(solution)/shard_map/psum | solution.py:151
  351.1 4.1 %scatter_custom_fusion.6 = f32[128,256]{1,0:T(8,128)S(1)} fusion(s32[512]{0:T(512)} %bitcast.142, f32[512,256]{1,0:T(8,128)} %fusion.21, f32[]{:T(128)} %constant.135.clone.1), kind=kCustom, calls=%fused_computation.123 | custom fusion | flops 131072 | bytes 131584 | tf_op jit(solution)/shard_map/while/body/eval_jaxpr/scatter-add | solution.py:38
  359.4 12.5 %all_gather.7 = bf16[1024,256]{0,1:T(8,128)(2,1)S(1)} all-gather(bf16[256,256]{0,1:T(8,128)(2,1)S(1)} %add_convert_fusion.2), channel_id=1, replica_groups=mesh['gx'=4,'gy'=8] {'gx'}, dimensions={0}, use_global_device_ids=true | all-gather | bytes 655360 | tf_op jit(solution)/shard_map/all_gather | solution.py:168
  372.0 9.1 %gather_fusion.5 = bf16[2048,256]{1,0:T(8,128)(2,1)} fusion(bf16[1024,256]{1,0:T(8,128)(2,1)S(1)} %copy.39, s32[2048]{0:T(1024)S(1)} %broadcast_clamp_fusion), kind=kCustom, calls=%fused_computation.11 | custom fusion | bytes 2105344 | tf_op jit(solution)/shard_map/jit(_take)/gather | solution.py:169
  381.1 2.3 copy.40
  383.4 2.5 add_convert_fusion
  385.9 2.3 copy.41
  (177 shorter events, 60.5 us)
Async XLA Ops:
  7.2 256.2 %reduce-scatter.2.cloned.1.call-start = ((), (), s32[]{:S(2)}) async-start(), calls=%async_computation.1 | async-start | bytes 655360 | tf_op jit(solution)/shard_map/reduce_scatter | solution.py:116
  12.6 63.0 %collective-permute-start = (bf16[512,256]{1,0:T(8,128)(2,1)}, bf16[512,256]{1,0:T(8,128)(2,1)}, u32[]{:S(2)}, u32[]{:S(2)}) collective-permute-start(bf16[512,256]{1,0:T(8,128)(2,1)} %broadcast_select_fusion.3), channel_id=1, source_target_pairs={{0,8},{8,16},{16,24},{1,9},{9,17},{17,25},{2,10},{10,18},{18,26},{... | collective-permute-start | bytes 786440 | tf_op jit(solution)/shard_map/ppermute | solution.py:12
  21.0 55.6 %collective-permute-start.1 = (bf16[512,256]{1,0:T(8,128)(2,1)}, bf16[512,256]{1,0:T(8,128)(2,1)}, u32[]{:S(2)}, u32[]{:S(2)}) collective-permute-start(bf16[512,256]{1,0:T(8,128)(2,1)} %broadcast_select_fusion.2), channel_id=1, source_target_pairs={{8,0},{16,8},{24,16},{9,1},{17,9},{25,17},{10,2},{18,10},{26,18},{... | collective-permute-start | bytes 786440 | tf_op jit(solution)/shard_map/ppermute | solution.py:12
  25.1 52.5 %collective-permute-start.2 = (bf16[512,256]{1,0:T(8,128)(2,1)}, bf16[512,256]{1,0:T(8,128)(2,1)}, u32[]{:S(2)}, u32[]{:S(2)}) collective-permute-start(bf16[512,256]{1,0:T(8,128)(2,1)} %broadcast_select_fusion.1), channel_id=1, source_target_pairs={{0,1},{1,2},{2,3},{3,4},{4,5},{5,6},{6,7},{8,9},{9,10},{10,11},{11... | collective-permute-start | bytes 786440 | tf_op jit(solution)/shard_map/ppermute | solution.py:12
  29.2 5.5 %copy-start.1 = (bf16[2048,256]{1,0:T(8,128)(2,1)S(1)}, bf16[2048,256]{1,0:T(8,128)(2,1)}, u32[]{:S(2)}) copy-start(bf16[2048,256]{1,0:T(8,128)(2,1)} %param.21) | copy-start | bytes 3145732
  30.1 48.5 %collective-permute-start.3 = (bf16[512,256]{1,0:T(8,128)(2,1)}, bf16[512,256]{1,0:T(8,128)(2,1)S(1)}, u32[]{:S(2)}, u32[]{:S(2)}) collective-permute-start(bf16[512,256]{1,0:T(8,128)(2,1)} %broadcast_select_fusion), channel_id=1, source_target_pairs={{1,0},{2,1},{3,2},{4,3},{5,4},{6,5},{7,6},{9,8},{10,9},{11,10},{12... | collective-permute-start | bytes 786440 | tf_op jit(solution)/shard_map/ppermute | solution.py:12
  33.0 5.6 %copy-start.23 = (s32[1,512]{1,0:T(1,128)S(1)}, s32[1,512]{1,0:T(1,128)}, u32[]{:S(2)}) copy-start(s32[1,512]{1,0:T(1,128)} %param.35) | copy-start | bytes 6148
  33.1 5.6 %copy-start.22 = (s32[1,512]{1,0:T(1,128)S(1)}, s32[1,512]{1,0:T(1,128)}, u32[]{:S(2)}) copy-start(s32[1,512]{1,0:T(1,128)} %param.34) | copy-start | bytes 6148
  33.1 6.7 %copy-start.29 = (f32[3,256]{1,0:T(4,128)S(1)}, f32[3,256]{1,0:T(4,128)}, u32[]{:S(2)}) copy-start(f32[3,256]{1,0:T(4,128)} %param.25) | copy-start | bytes 9220
  33.1 7.3 %copy-start.20 = (s32[2048,1]{0,1:T(1,128)S(1)}, s32[2048,1]{0,1:T(1,128)}, u32[]{:S(2)}) copy-start(s32[2048,1]{0,1:T(1,128)} %param.29) | copy-start | bytes 24580
  33.1 7.3 %copy-start.21 = (s32[2048]{0:T(1024)S(1)}, s32[2048]{0:T(1024)}, u32[]{:S(2)}) copy-start(s32[2048]{0:T(1024)} %param.30) | copy-start | bytes 24580
  33.1 22.6 %copy-start.30 = (s32[1,256]{1,0:T(1,128)S(1)}, s32[1,256]{1,0:T(1,128)}, u32[]{:S(2)}) copy-start(s32[1,256]{1,0:T(1,128)} %param.33) | copy-start | bytes 3076
  33.1 24.9 %copy-start.12 = (s32[1,1024]{1,0:T(1,128)S(1)}, s32[1,1024]{1,0:T(1,128)}, u32[]{:S(2)}) copy-start(s32[1,1024]{1,0:T(1,128)} %param.32) | copy-start | bytes 12292
  34.7 39.5 %copy-start.35 = (u32[32]{0:T(128)S(1)}, u32[32]{0:T(128)}, u32[]{:S(2)}) copy-start(u32[32]{0:T(128)} %constant.209) | copy-start | bytes 388
  41.0 37.6 %copy-start.10 = (s32[2048]{0:T(1024)}, s32[2048]{0:T(1024)S(1)}, u32[]{:S(2)}) copy-start(s32[2048]{0:T(1024)S(1)} %get-tuple-element.111) | copy-start | bytes 24580
  55.7 22.9 %copy-start.26 = (s32[256,1]{0,1:T(1,128)}, s32[256,1]{0,1:T(1,128)S(1)}, u32[]{:S(2)}) copy-start(s32[256,1]{0,1:T(1,128)S(1)} %compare_select_fusion.10) | copy-start | bytes 3076
  75.6 4.5 %copy-start.3 = (s32[1,1,8192]{2,1,0:T(1,128)S(1)}, s32[1,1,8192]{2,1,0:T(1,128)}, u32[]{:S(2)}) copy-start(s32[1,1,8192]{2,1,0:T(1,128)} %param.28) | copy-start | bytes 98308
  75.6 4.5 %copy-start.4 = (s32[1,1,8192]{2,1,0:T(1,128)S(1)}, s32[1,1,8192]{2,1,0:T(1,128)}, u32[]{:S(2)}) copy-start(s32[1,1,8192]{2,1,0:T(1,128)} %param.27) | copy-start | bytes 98308
  98.3 17.8 %copy-start.6 = (bf16[256,256]{1,0:T(8,128)(2,1)S(1)}, bf16[256,256]{1,0:T(8,128)(2,1)}, u32[]{:S(2)}) copy-start(bf16[256,256]{1,0:T(8,128)(2,1)} %get-tuple-element.236) | copy-start | bytes 393220 | tf_op jit(solution)/shard_map/while
  163.9 17.8 %copy-start.6 = (bf16[256,256]{1,0:T(8,128)(2,1)S(1)}, bf16[256,256]{1,0:T(8,128)(2,1)}, u32[]{:S(2)}) copy-start(bf16[256,256]{1,0:T(8,128)(2,1)} %get-tuple-element.236) | copy-start | bytes 393220 | tf_op jit(solution)/shard_map/while
  221.1 16.0 %copy-start.9 = (s32[1,1024]{1,0:T(1,128)S(1)}, s32[1,1024]{1,0:T(1,128)}, u32[]{:S(2)}) copy-start(s32[1,1024]{1,0:T(1,128)} %param.31) | copy-start | bytes 12292
  221.1 16.0 %copy-start.14 = (s32[1,1024]{1,0:T(1,128)S(1)}, s32[1,1024]{1,0:T(1,128)}, u32[]{:S(2)}) copy-start(s32[1,1024]{1,0:T(1,128)} %broadcast_clamp_fusion.3) | copy-start | bytes 12292
  221.1 16.0 %copy-start.15 = (s32[1,1024]{1,0:T(1,128)S(1)}, s32[1,1024]{1,0:T(1,128)}, u32[]{:S(2)}) copy-start(s32[1,1024]{1,0:T(1,128)} %broadcast_minimum_fusion) | copy-start | bytes 12292
  221.1 16.1 %copy-start.13 = (s32[1,1024]{1,0:T(1,128)S(1)}, s32[1,1024]{1,0:T(1,128)}, u32[]{:S(2)}) copy-start(s32[1,1024]{1,0:T(1,128)} %param.32) | copy-start | bytes 12292
  221.1 16.1 %copy-start.16 = (s32[1024,1]{0,1:T(1,128)S(1)}, s32[1024,1]{0,1:T(1,128)}, u32[]{:S(2)}) copy-start(s32[1024,1]{0,1:T(1,128)} %compare_select_fusion.4) | copy-start | bytes 12292
  236.3 106.4 %all-reduce.4.cloned.1.call-start = ((), (), s32[]{:S(2)}) async-start(), calls=%async_computation.2 | async-start | bytes 131072 | tf_op jit(solution)/shard_map/psum | solution.py:151
  287.8 10.0 %copy-start.25 = (f32[1,256]{1,0:T(1,128)S(1)}, f32[1,256]{1,0:T(1,128)}, u32[]{:S(2)}) copy-start(f32[1,256]{1,0:T(1,128)} %get-tuple-element.123) | copy-start | bytes 3076
  294.4 48.3 %copy-start.32 = (f32[128]{0:T(128)S(1)}, f32[128]{0:T(128)}, u32[]{:S(2)}) copy-start(f32[128]{0:T(128)} %convert_maximum_fusion.1) | copy-start | bytes 1540
  296.3 47.6 %copy-start.18 = (s32[1024]{0:T(1024)S(1)}, s32[1024]{0:T(1024)}, u32[]{:S(2)}) copy-start(s32[1024]{0:T(1024)} %get-tuple-element.135) | copy-start | bytes 12292
  298.1 48.9 %copy-start.17 = (s32[1024]{0:T(1024)S(1)}, s32[1024]{0:T(1024)}, u32[]{:S(2)}) copy-start(s32[1024]{0:T(1024)} %get-tuple-element.134) | copy-start | bytes 12292
  349.0 8.9 %copy-start.24 = (f32[1,256]{1,0:T(1,128)S(1)}, f32[1,256]{1,0:T(1,128)}, u32[]{:S(2)}) copy-start(f32[1,256]{1,0:T(1,128)} %get-tuple-element.121) | copy-start | bytes 3076
  351.1 8.2 %copy-start.31 = (pred[256]{0:T(512)(128)(4,1)S(1)}, pred[256]{0:T(512)(128)(4,1)}, u32[]{:S(2)}) copy-start(pred[256]{0:T(512)(128)(4,1)} %compare_and_fusion.11) | copy-start | bytes 772
  (11 other events, 31.3 us)
Sparse Core Ops, SparseCore 0:
  236.4 26.8 reduce-scatter.1
  300.9 41.8 all-reduce.3
where the time goes:
time: 397 us; the launch traced here: 396 us
  local copies, waits for them, and re-layouts  122 us (31%)
  other arithmetic  107 us (27%)
  waiting for transfers between devices  68.2 us (17%)
  matrix products  37.3 us (9%)
  blocking collectives  34.5 us (9%)
  between operations  15.5 us (4%)
  starting transfers between devices  10.4 us (3%)
    scatter-add x4, other arithmetic, advance(): return (summed.at[targets].add(message, mode='drop'), None)  57.9 us
    psum x1, waiting for transfers between devices, body(): lax.psum(partial_top.astype(jnp.bfloat16), 'gx').astype(jnp.float32)  42 us
    gather x4, local copies, waits for them, and re-layouts, advance(): jnp.take(receiver_term, jnp.minimum(targets, count - 1), axis=0)  40.8 us
    gather x3, local copies, waits for them, and re-layouts, fetch(): return jnp.take(table, picked, axis=0).astype(jnp.float32)  37.4 us
    reduce_scatter x1, waiting for transfers between devices, body(): lax.psum_scatter(partial_value.astype(jnp.bfloat16), 'gx', scatter_dimens...  26.1 us
    dot_general x4, matrix products, advance(): message = jnp.dot(hidden, weight_out, preferred_element_type=jnp.float32)  17 us
    scatter-add x1, other arithmetic, body(): jnp.zeros((members * coarse_rows,), jnp.float32).at[parent].add(1.0)  14.7 us
    scatter-add x1, other arithmetic, body(): partial_value = jnp.zeros((members * coarse_rows, width), jnp.float32).at...  13 us
  transfers between devices with their start and end apart: 6, of which 2 were waited for; matrix products, arithmetic and copies ran while one was open for 11% of the time, Pallas kernels for 0%

commit v1 on v0

v1 whole, which is shorter than its diff:
```python
import functools

import jax
import jax.numpy as jnp
from jax import lax
from jax.experimental import pallas as pl
from jax.experimental.pallas import tpu as pltpu
from jax.sharding import PartitionSpec as P

F32 = jnp.float32
BF16 = jnp.bfloat16
LANES = 128
PAD = 8
CHUNK = 512
ROWS = 256
VMEM_LIMIT = 56 << 20

SMEM_SPEC = pl.BlockSpec(memory_space=pltpu.SMEM)
VMEM_SPEC = pl.BlockSpec(memory_space=pltpu.VMEM)


def shifted(block, axis, distance, wrap):
    count = lax.axis_size(axis)
    route = []
    for i in range(count):
        j = i + distance
        if wrap:
            route.append((i, j % count))
        elif 0 <= j < count:
            route.append((i, j))
    return lax.ppermute(block, axis, route)


def dot(a, b):
    return jnp.dot(a, b, preferred_element_type=F32)


def silu(v):
    return (0.5 * v) * (1.0 + jnp.tanh(0.5 * v))


def put_rows(table, stride, begin, rows, values):
    table[begin : begin + rows, :] = values[:, :LANES]
    table[stride + begin : stride + begin + rows, :] = values[:, LANES:]


def project_into(table, stride, begin, states, weight):
    rows = states.shape[0]
    step = min(rows, 512)
    for at in range(0, rows, step):
        term = dot(states[at : at + step, :], weight).astype(BF16).astype(F32)
        put_rows(table, stride, begin + at, step, term)


def selection(indices, begin, rows):
    columns = indices.shape[1]
    number = lax.broadcasted_iota(jnp.int32, (rows, columns), 0) + begin
    return jnp.where(number == indices, 1.0, 0.0).astype(BF16)


def gather_chunk(c, chunk, s_ref, r_ref, ts, s_stride, tr, r_stride, buf):
    base = c * chunk
    for j in range(chunk):
        s = s_ref[base + j]
        r = r_ref[base + j]
        buf[pl.ds(j, 2, stride=chunk + PAD), :] = (
            ts[pl.ds(s, 2, stride=s_stride), :] + tr[pl.ds(r, 2, stride=r_stride), :]
        )


def edge_sums(nodes, edges, s_ref, r_ref, rv_ref, ts, s_stride, tr, r_stride, buf, hid, acc):
    chunk = rv_ref.shape[1]
    turns = edges // chunk
    block = min(ROWS, nodes)
    acc[0:nodes, :] = jnp.zeros((nodes, 2 * LANES), F32)

    def gather(c):
        gather_chunk(c, chunk, s_ref, r_ref, ts, s_stride, tr, r_stride, buf)

    def activate():
        hid[0:chunk, :LANES] = silu(buf[0:chunk, :]).astype(BF16)
        hid[0:chunk, LANES:] = silu(buf[chunk + PAD : 2 * chunk + PAD, :]).astype(BF16)

    def add(c):
        targets = rv_ref[pl.ds(c, 1), :]
        hidden = hid[0:chunk, :]
        for at in range(0, nodes, block):
            acc[at : at + block, :] += dot(selection(targets, at, block), hidden)

    gather(0)

    def turn(c, carry):
        activate()
        gather(c + 1)
        add(c)
        return carry

    if turns > 1:
        lax.fori_loop(0, turns - 1, turn, 0)
    activate()
    add(turns - 1)


def updated(states, summed, w_ref, gain):
    aggregate = dot(summed.astype(BF16), w_ref[2]).astype(BF16)
    inner = silu(dot(states, w_ref[3]) + dot(aggregate, w_ref[4])).astype(BF16)
    output = dot(inner, w_ref[5])
    centred = output - jnp.mean(output, axis=1, keepdims=True)
    spread = jnp.mean(centred * centred, axis=1, keepdims=True)
    return states.astype(F32) + gain * centred * lax.rsqrt(spread + 1e-05)


def halo_kernel(l_ref, nodes, *refs):
    outs, (table, buf) = refs[:4], refs[4:]
    rows = nodes.shape[0]
    listed = outs[0].shape[0]
    unroll = 64
    put_rows(table, rows + PAD, 0, rows, nodes[...].astype(F32))
    for d in range(4):

        def some(c, carry):
            base = pl.multiple_of(c * unroll, unroll)
            for j in range(unroll):
                i = l_ref[d * listed + base + j]
                buf[pl.ds(base + j, 2, stride=listed + PAD), :] = table[
                    pl.ds(i, 2, stride=rows + PAD), :
                ]
            return carry

        lax.fori_loop(0, listed // unroll, some, 0)
        outs[d][:, :LANES] = buf[0:listed, :].astype(BF16)
        outs[d][:, LANES:] = buf[listed + PAD : 2 * listed + PAD, :].astype(BF16)


def count_kernel(members, p_ref, out):
    size = out.shape[1]
    eye = lax.broadcasted_iota(jnp.int32, (size, size), 0) == lax.broadcasted_iota(
        jnp.int32, (size, size), 1
    )
    parents = p_ref[...]
    for d in range(members):
        chosen = jnp.where(
            lax.broadcasted_iota(jnp.int32, (size, parents.shape[1]), 0) + d * size == parents,
            1.0,
            0.0,
        )
        column = jnp.sum(chosen, axis=1, keepdims=True)
        row = jnp.sum(jnp.where(eye, column, 0.0), axis=0, keepdims=True)
        out[d : d + 1, :] = row.astype(jnp.int32)


def fine_kernel(members, s_ref, r_ref, rv_ref, p_ref, nodes, h0, h1, h2, h3, w_ref, g_ref, *refs):
    one, parts = refs[0], refs[1 : 1 + members]
    ts, tr, buf, hid, acc = refs[1 + members :]
    count = nodes.shape[0]
    edges = s_ref.shape[0]
    listed = h0.shape[0]
    s_stride = count + 4 * listed + PAD
    r_stride = count + PAD
    project_into(ts, s_stride, 0, nodes, w_ref[0])
    for d, halo in enumerate((h0, h1, h2, h3)):
        project_into(ts, s_stride, count + d * listed, halo, w_ref[0])
    project_into(tr, r_stride, 0, nodes, w_ref[1])
    put_rows(tr, r_stride, count, PAD, jnp.zeros((PAD, 2 * LANES), F32))
    edge_sums(count, edges, s_ref, r_ref, rv_ref, ts, s_stride, tr, r_stride, buf, hid, acc)
    gain = g_ref[0:1, :]
    step = 512
    for at in range(0, count, step):
        rows = slice(at, at + step)
        one[rows, :] = updated(nodes[rows, :], acc[rows, :], w_ref, gain).astype(BF16)
    parents = p_ref[...]
    size = parts[0].shape[0]
    for d in range(members):
        parts[d][...] = dot(selection(parents, d * size, size), one[...]).astype(BF16)


def mean_kernel(members, c_ref, *refs):
    pieces, out = refs[:members], refs[members]
    size = out.shape[0]
    eye = lax.broadcasted_iota(jnp.int32, (size, size), 0) == lax.broadcasted_iota(
        jnp.int32, (size, size), 1
    )
    total = pieces[0][...].astype(F32)
    for piece in pieces[1:]:
        total = total + piece[...].astype(F32)
    children = jnp.sum(c_ref[...].astype(F32), axis=0, keepdims=True)
    column = jnp.sum(jnp.where(eye, children, 0.0), axis=1, keepdims=True)
    out[...] = (total / jnp.maximum(column, 1.0)).astype(BF16)


def turned(row):
    n = row.shape[1]
    return jnp.concatenate(
        [
            jnp.transpose(jnp.broadcast_to(row[:, at : at + LANES], (LANES, LANES)))
            for at in range(0, n, LANES)
        ],
        axis=0,
    )


def picks(row, columns):
    column = turned(row)
    lane = lax.broadcasted_iota(jnp.int32, column.shape, 1)
    return jnp.concatenate(
        [
            jnp.where(column == lane + at, 1.0, 0.0).astype(BF16)
            for at in range(0, columns, LANES)
        ],
        axis=1,
    )


def upper_kernel(
    members,
    cs_ref,
    cr_ref,
    crv_ref,
    ts_ref,
    tr_ref,
    trv_ref,
    tp_ref,
    p_ref,
    fine,
    cw_ref,
    tw_ref,
    g_ref,
    *refs,
):
    pieces = refs[:members]
    fine_out, coarse_out = refs[members : members + 2]
    ts, tr, buf, hid, acc, zero, one = refs[members + 2 :]
    size = pieces[0].shape[0]
    count = size * members
    tops = count // 8
    stride = count + PAD
    for d in range(members):
        zero[d * size : (d + 1) * size, :] = pieces[d][...]
    project_into(ts, stride, 0, zero, cw_ref[0])
    project_into(tr, stride, 0, zero, cw_ref[1])
    edge_sums(
        count, cs_ref.shape[0], cs_ref, cr_ref, crv_ref, ts, stride, tr, stride, buf, hid, acc
    )
    gain = g_ref[1:2, :]
    step = min(count, 512)
    for at in range(0, count, step):
        rows = slice(at, at + step)
        one[rows, :] = updated(zero[rows, :], acc[rows, :], cw_ref, gain).astype(BF16)
    chosen = jnp.where(
        lax.broadcasted_iota(jnp.int32, (tops, count), 0) == tp_ref[...], 1.0, 0.0
    )
    held = jnp.sum(chosen, axis=1, keepdims=True)
    top_zero = (dot(chosen.astype(BF16), one[...]) / jnp.maximum(held, 1.0)).astype(BF16)
    top_stride = tops + PAD
    put_rows(ts, top_stride, 0, tops, dot(top_zero, tw_ref[0]).astype(BF16).astype(F32))
    put_rows(tr, top_stride, 0, tops, dot(top_zero, tw_ref[1]).astype(BF16).astype(F32))
    edge_sums(
        tops, ts_ref.shape[0], ts_ref, tr_ref, trv_ref, ts, top_stride, tr, top_stride, buf, hid, acc
    )
    top_one = updated(top_zero, acc[0:tops, :], tw_ref, g_ref[2:3, :]).astype(BF16)
    for at in range(0, count, size):
        rows = slice(at, at + size)
        lifted = dot(picks(tp_ref[:, rows], tops), top_one)
        one[rows, :] = (one[rows, :].astype(F32) + lifted).astype(BF16)
    coarse_out[...] = one[0:size, :]
    for at in range(0, fine.shape[0], ROWS):
        rows = slice(at, at + ROWS)
        lifted = dot(picks(p_ref[:, rows], count), one[...])
        fine_out[rows, :] = (fine[rows, :].astype(F32) + lifted).astype(BF16)


def call(kernel, outs, specs, scratch, *operands):
    return pl.pallas_call(
        kernel,
        out_shape=outs,
        in_specs=specs,
        out_specs=jax.tree.map(lambda _: VMEM_SPEC, outs),
        scratch_shapes=scratch,
        compiler_params=pltpu.CompilerParams(vmem_limit_bytes=VMEM_LIMIT),
    )(*operands)


def body(
    fine_nodes,
    fine_weights,
    coarse_weights,
    top_weights,
    gains,
    send_list,
    fine_sender,
    fine_receiver,
    pool_owner,
    pool_local,
    coarse_sender,
    coarse_receiver,
    top_parent,
    top_sender,
    top_receiver,
):
    nodes, width = fine_nodes.shape
    members = lax.axis_size("gx")
    me = lax.axis_index("gx")
    size = nodes // 8
    count = size * members
    tops = count // 8
    listed = send_list.shape[-1]
    edges = fine_sender.shape[-1]
    shape = jax.ShapeDtypeStruct

    halo = call(
        halo_kernel,
        [shape((listed, width), BF16)] * 4,
        [SMEM_SPEC, VMEM_SPEC],
        [
            pltpu.VMEM((2 * (nodes + PAD), LANES), F32),
            pltpu.VMEM((2 * (listed + PAD), LANES), F32),
        ],
        send_list.reshape(-1),
        fine_nodes,
    )
    arrived = [
        shifted(halo[slot], axis, distance, False)
        for slot, (axis, distance) in enumerate((("gx", 1), ("gx", -1), ("gy", 1), ("gy", -1)))
    ]

    owner = pool_owner.reshape(1, -1)
    local = pool_local.reshape(1, -1)
    ahead = lax.rem(owner - me + members, members) * size + local
    behind = lax.rem(me - owner + members, members) * size + local
    counts = call(
        functools.partial(count_kernel, members),
        shape((members, size), jnp.int32),
        [VMEM_SPEC],
        [],
        ahead,
    )
    share = jnp.concatenate(
        [coarse_sender.reshape(1, -1), coarse_receiver.reshape(1, -1), top_parent.reshape(1, -1)],
        axis=1,
    )
    mixed = [
        jnp.concatenate([share, counts[d : d + 1]], axis=1) for d in range(members)
    ]
    mixed = [mixed[0]] + [shifted(mixed[d], "gx", d, True) for d in range(1, members)]
    per = coarse_sender.shape[-1]
    senders = jnp.concatenate([piece[0, :per] for piece in mixed])
    senders = lax.rem(me - senders // size + members, members) * size + lax.rem(senders, size)
    receivers = jnp.concatenate([piece[0, per : 2 * per] + d * size for d, piece in enumerate(mixed)])
    tops_of = jnp.concatenate([piece[:, 2 * per : 2 * per + size] for piece in mixed], axis=1)
    children = jnp.concatenate([piece[:, 2 * per + size :] for piece in mixed], axis=0)

    chunk = min(CHUNK, edges)
    fine_one, *parts = call(
        functools.partial(fine_kernel, members),
        [shape((nodes, width), BF16)] + [shape((size, width), BF16)] * members,
        [SMEM_SPEC] * 2 + [VMEM_SPEC] * 9,
        [
            pltpu.VMEM((2 * (nodes + 4 * listed + PAD), LANES), F32),
            pltpu.VMEM((2 * (nodes + PAD), LANES), F32),
            pltpu.VMEM((2 * (chunk + PAD), LANES), F32),
            pltpu.VMEM((chunk, width), BF16),
            pltpu.VMEM((nodes, width), F32),
        ],
        fine_sender.reshape(-1),
        fine_receiver.reshape(-1),
        fine_receiver.reshape(-1, chunk),
        ahead,
        fine_nodes,
        *arrived,
        fine_weights,
        gains,
    )
    parts = [parts[0]] + [shifted(parts[d], "gx", d, True) for d in range(1, members)]
    zero = call(
        functools.partial(mean_kernel, members),
        shape((size, width), BF16),
        [VMEM_SPEC] * (1 + members),
        [],
        children,
        *parts,
    )
    zeros = [zero] + [shifted(zero, "gx", d, True) for d in range(1, members)]

    top_edges = top_sender.shape[-1]
    chunk = min(CHUNK, per * members, top_edges)
    fine_state, coarse_state = call(
        functools.partial(upper_kernel, members),
        [shape((nodes, width), BF16), shape((size, width), BF16)],
        [SMEM_SPEC] * 2 + [VMEM_SPEC] + [SMEM_SPEC] * 2 + [VMEM_SPEC] * (7 + members),
        [
            pltpu.VMEM((2 * (count + PAD), LANES), F32),
            pltpu.VMEM((2 * (count + PAD), LANES), F32),
            pltpu.VMEM((2 * (chunk + PAD), LANES), F32),
            pltpu.VMEM((chunk, width), BF16),
            pltpu.VMEM((count, width), F32),
            pltpu.VMEM((count, width), BF16),
            pltpu.VMEM((count, width), BF16),
        ],
        senders,
        receivers,
        receivers.reshape(-1, chunk),
        top_sender.reshape(-1),
        top_receiver.reshape(-1),
        top_receiver.reshape(-1, chunk),
        tops_of,
        behind,
        fine_one,
        coarse_weights,
        top_weights,
        gains,
        *zeros,
    )
    return (fine_state, coarse_state[None])


def solution(mesh):
    placed = (
        P(("gx", "gy"), None),
        P(),
        P(),
        P(),
        P(),
        P("gx", "gy", None, None),
        P("gx", "gy", None),
        P("gx", "gy", None),
        P(("gx", "gy"), None),
        P(("gx", "gy")),
        P("gy", "gx"),
        P("gy", "gx"),
        P("gy", "gx"),
        P("gy", None),
        P("gy", None),
    )
    return jax.shard_map(
        body,
        mesh=mesh,
        in_specs=placed,
        out_specs=(P(("gx", "gy"), None), P("gy", "gx", None)),
        check_vma=False,
    )
```

time: 397 us -> 99.9 us (0.25)
  the two profiles are of different devices: /device:TPU:0 before, /device:TPU:16 now
where the time goes in v1:
time: 99.9 us; the launch traced here: 99.5 us
  Pallas kernels  50.8 us (51%)
  starting transfers between devices  23.9 us (24%)
  waiting for transfers between devices  12.7 us (13%)
  other arithmetic  5.81 us (6%)
  local copies, waits for them, and re-layouts  5.39 us (5%)
    pallas_call x5, Pallas kernels, call(): pl.pallas_call(kernel, out_shape=outs, in_specs=specs, out_specs=jax.tree...  50.8 us
    ppermute x13, starting transfers between devices, shifted(): return lax.ppermute(block, axis, route)  23.9 us
    ppermute x13, waiting for transfers between devices, shifted(): return lax.ppermute(block, axis, route)  12.7 us
    unnamed x34, local copies, waits for them, and re-layouts  3.9 us
  transfers between devices with their start and end apart: 13, of which 7 were waited for; matrix products, arithmetic and copies ran while one was open for 6% of the time, Pallas kernels for 5%

profile of v1, /device:TPU:16, one launch (start us, length us, event | category | flops | bytes accessed | tf_op | source)
XLA Modules:
  0.0 99.5 jit_solution(5757536814706314216)
XLA Ops:
  0.6 0.7 subtract_add_fusion
  1.4 0.6 fusion.12
  2.0 2.2 %shard_map.158 = s32[4,256]{1,0:T(4,128)} custom-call(s32[1,2048]{1,0:T(1,128)} %bitcast.20), custom_call_target="tpu_custom_call" | custom-call | tf_op jit(solution)/shard_map/pallas_call | solution.py:273
  4.2 0.8 fusion.19
  5.1 0.7 copy-done.15
  5.8 2.5 %collective-permute-start.2 = (s32[1,2560]{1,0:T(1,128)S(1)}, s32[1,2560]{1,0:T(1,128)S(1)}, u32[]{:S(2)}, u32[]{:S(2)}) collective-permute-start(s32[1,2560]{1,0:T(1,128)S(1)} %get-tuple-element.42), channel_id=1, source_target_pairs={{0,24},{8,0},{16,8},{24,16},{1,25},{9,1},{17,9},{25,17},{2,26},{10... | collective-permute-start | bytes 30728 | tf_op jit(solution)/shard_map/ppermute | solution.py:31
  10.0 4.7 %shard_map.159 = (bf16[512,256]{1,0:T(8,128)(2,1)}, bf16[512,256]{1,0:T(8,128)(2,1)}, bf16[512,256]{1,0:T(8,128)(2,1)}, bf16[512,256]{1,0:T(8,128)(2,1)}) custom-call(s32[2048]{0:T(1024)} %bitcast.25, bf16[2048,256]{1,0:T(8,128)(2,1)} %nodes.3), custom_call_target="tpu_custom_call" | custom-call | tf_op jit(solution)/shard_map/pallas_call | solution.py:273
  14.7 4.3 %collective-permute-start.3 = (bf16[512,256]{1,0:T(8,128)(2,1)}, bf16[512,256]{1,0:T(8,128)(2,1)S(1)}, u32[]{:S(2)}, u32[]{:S(2)}) collective-permute-start(bf16[512,256]{1,0:T(8,128)(2,1)} %get-tuple-element.13), channel_id=1, source_target_pairs={{0,8},{8,16},{16,24},{1,9},{9,17},{17,25},{2,10},{10,18},{18,26},{... | collective-permute-start | bytes 786440 | tf_op jit(solution)/shard_map/ppermute | solution.py:31
  19.0 1.3 %collective-permute-start.4 = (bf16[512,256]{1,0:T(8,128)(2,1)}, bf16[512,256]{1,0:T(8,128)(2,1)S(1)}, u32[]{:S(2)}, u32[]{:S(2)}) collective-permute-start(bf16[512,256]{1,0:T(8,128)(2,1)} %get-tuple-element.14), channel_id=1, source_target_pairs={{8,0},{16,8},{24,16},{9,1},{17,9},{25,17},{10,2},{18,10},{26,18},{... | collective-permute-start | bytes 786440 | tf_op jit(solution)/shard_map/ppermute | solution.py:31
  20.8 0.7 reduce.18
  21.5 0.7 reduce.19
  22.2 0.6 reshape.79.rv_ref
  22.8 1.9 %collective-permute-start.5 = (bf16[512,256]{1,0:T(8,128)(2,1)}, bf16[512,256]{1,0:T(8,128)(2,1)S(1)}, u32[]{:S(2)}, u32[]{:S(2)}) collective-permute-start(bf16[512,256]{1,0:T(8,128)(2,1)} %get-tuple-element.15), channel_id=1, source_target_pairs={{0,1},{1,2},{2,3},{3,4},{4,5},{5,6},{6,7},{8,9},{9,10},{10,11},{11... | collective-permute-start | bytes 786440 | tf_op jit(solution)/shard_map/ppermute | solution.py:31
  24.8 3.6 %collective-permute-start.6 = (bf16[512,256]{1,0:T(8,128)(2,1)}, bf16[512,256]{1,0:T(8,128)(2,1)S(1)}, u32[]{:S(2)}, u32[]{:S(2)}) collective-permute-start(bf16[512,256]{1,0:T(8,128)(2,1)} %get-tuple-element.16), channel_id=1, source_target_pairs={{1,0},{2,1},{3,2},{4,3},{5,4},{6,5},{7,6},{9,8},{10,9},{11,10},{12... | collective-permute-start | bytes 786440 | tf_op jit(solution)/shard_map/ppermute | solution.py:31
  28.5 0.6 pad_add_fusion.1.cr_ref
  29.1 1.1 %collective-permute-done.4.h1 = bf16[512,256]{1,0:T(8,128)(2,1)S(1)} collective-permute-done((bf16[512,256]{1,0:T(8,128)(2,1)}, bf16[512,256]{1,0:T(8,128)(2,1)S(1)}, u32[]{:S(2)}, u32[]{:S(2)}) %collective-permute-start.4) | collective-permute-done | bytes 262176 | tf_op jit(solution)/shard_map/ppermute | solution.py:31
  30.7 1.9 %collective-permute-done.6.h3 = bf16[512,256]{1,0:T(8,128)(2,1)S(1)} collective-permute-done((bf16[512,256]{1,0:T(8,128)(2,1)}, bf16[512,256]{1,0:T(8,128)(2,1)S(1)}, u32[]{:S(2)}, u32[]{:S(2)}) %collective-permute-start.6) | collective-permute-done | bytes 262176 | tf_op jit(solution)/shard_map/ppermute | solution.py:31
  32.6 0.7 copy-done.3
  33.3 26.2 %shard_map.160 = (bf16[2048,256]{1,0:T(8,128)(2,1)}, bf16[256,256]{1,0:T(8,128)(2,1)}, bf16[256,256]{1,0:T(8,128)(2,1)}, bf16[256,256]{1,0:T(8,128)(2,1)}, bf16[256,256]{1,0:T(8,128)(2,1)}) custom-call(s32[8192]{0:T(1024)} %bitcast.23, s32[8192]{0:T(1024)} %bitcast.19, s32[16,512]{1,0:T(8,128)} %reshape.79.rv_ref, s32[1,2048]{1,0:T(1,128)} %bitcast.21, ...), custom_call_target="tpu_custom_call" | custom-call | tf_op jit(solution)/shard_map/pallas_call | solution.py:273
  59.5 2.7 %collective-permute-start.7 = (bf16[256,256]{1,0:T(8,128)(2,1)}, bf16[256,256]{1,0:T(8,128)(2,1)S(1)}, u32[]{:S(2)}, u32[]{:S(2)}) collective-permute-start(bf16[256,256]{1,0:T(8,128)(2,1)} %get-tuple-element.19), channel_id=1, source_target_pairs={{0,8},{8,16},{16,24},{24,0},{1,9},{9,17},{17,25},{25,1},{2,10},{10... | collective-permute-start | bytes 393224 | tf_op jit(solution)/shard_map/ppermute | solution.py:31
  62.7 1.9 %collective-permute-start.9 = (bf16[256,256]{1,0:T(8,128)(2,1)}, bf16[256,256]{1,0:T(8,128)(2,1)S(1)}, u32[]{:S(2)}, u32[]{:S(2)}) collective-permute-start(bf16[256,256]{1,0:T(8,128)(2,1)} %get-tuple-element.21), channel_id=1, source_target_pairs={{0,24},{8,0},{16,8},{24,16},{1,25},{9,1},{17,9},{25,17},{2,26},{10... | collective-permute-start | bytes 393224 | tf_op jit(solution)/shard_map/ppermute | solution.py:31
  65.2 0.6 pad_add_fusion.2.crv_ref
  66.2 3.5 %collective-permute-done.8.refs_2_ = bf16[256,256]{1,0:T(8,128)(2,1)S(1)} collective-permute-done((bf16[256,256]{1,0:T(8,128)(2,1)}, bf16[256,256]{1,0:T(8,128)(2,1)S(1)}, u32[]{:S(2)}, u32[]{:S(2)}) %collective-permute-start.8) | collective-permute-done | bytes 131104 | tf_op jit(solution)/shard_map/ppermute | solution.py:31
  69.8 0.6 copy-done.8
  70.4 1.9 %shard_map.161.refs_0_ = bf16[256,256]{1,0:T(8,128)(2,1)} custom-call(s32[4,256]{1,0:T(4,128)} %pad_add_fusion.8.c_ref, bf16[256,256]{1,0:T(8,128)(2,1)} %get-tuple-element.18.refs_0_, bf16[256,256]{1,0:T(8,128)(2,1)} %copy-done.6, bf16[256,256]{1,0:T(8,128)(2,1)} %copy-done.8, bf16[256,256]{1,0:T(8,128)(2,1)} %copy-done.10), custom_call_target="tpu_custom_call" | custom-call | tf_op jit(solution)/shard_map/pallas_call | solution.py:273
  72.3 2.2 %collective-permute-start.12 = (bf16[256,256]{1,0:T(8,128)(2,1)}, bf16[256,256]{1,0:T(8,128)(2,1)S(1)}, u32[]{:S(2)}, u32[]{:S(2)}) collective-permute-start(bf16[256,256]{1,0:T(8,128)(2,1)} %shard_map.161.refs_0_), channel_id=1, source_target_pairs={{0,24},{8,0},{16,8},{24,16},{1,25},{9,1},{17,9},{25,17},{2,26},{10... | collective-permute-start | bytes 393224 | tf_op jit(solution)/shard_map/ppermute | solution.py:31
  74.6 1.5 %collective-permute-start.11 = (bf16[256,256]{1,0:T(8,128)(2,1)}, bf16[256,256]{1,0:T(8,128)(2,1)S(1)}, u32[]{:S(2)}, u32[]{:S(2)}) collective-permute-start(bf16[256,256]{1,0:T(8,128)(2,1)} %shard_map.161.refs_0_), channel_id=1, source_target_pairs={{0,16},{8,24},{16,0},{24,8},{1,17},{9,25},{17,1},{25,9},{2,18},{10... | collective-permute-start | bytes 393224 | tf_op jit(solution)/shard_map/ppermute | solution.py:31
  77.1 0.6 fusion.4.cs_ref
  77.7 1.3 %collective-permute-done.12.refs_3_ = bf16[256,256]{1,0:T(8,128)(2,1)S(1)} collective-permute-done((bf16[256,256]{1,0:T(8,128)(2,1)}, bf16[256,256]{1,0:T(8,128)(2,1)S(1)}, u32[]{:S(2)}, u32[]{:S(2)}) %collective-permute-start.12) | collective-permute-done | bytes 131104 | tf_op jit(solution)/shard_map/ppermute | solution.py:31
  79.0 4.0 %collective-permute-done.11.refs_2_ = bf16[256,256]{1,0:T(8,128)(2,1)S(1)} collective-permute-done((bf16[256,256]{1,0:T(8,128)(2,1)}, bf16[256,256]{1,0:T(8,128)(2,1)S(1)}, u32[]{:S(2)}, u32[]{:S(2)}) %collective-permute-start.11) | collective-permute-done | bytes 131104 | tf_op jit(solution)/shard_map/ppermute | solution.py:31
  83.0 0.6 copy-done.7
  83.6 15.8 %shard_map.162 = (bf16[2048,256]{1,0:T(8,128)(2,1)}, bf16[256,256]{1,0:T(8,128)(2,1)}) custom-call(s32[4096]{0:T(1024)} %fusion.4.cs_ref, s32[4096]{0:T(1024)} %pad_add_fusion.1.cr_ref, s32[8,512]{1,0:T(8,128)} %pad_add_fusion.2.crv_ref, s32[512]{0:T(512)} %bitcast.37, s32[512]{0:T(512)} %bitcast.36, s32[1,512]{1,0:T(1,128)} %trv_ref.1, ...), custom_call_target="tpu_custom_call" | custom-call | tf_op jit(solution)/shard_map/pallas_call | solution.py:273
  (55 shorter events, 5.5 us)
Async XLA Ops:
  0.6 0.7 copy-start.13
  4.2 0.8 copy-start.11
  4.2 0.9 copy-start.12
  5.1 0.7 copy-start.15
  5.8 3.6 %copy-start.14 = (s32[1,1,4,512]{3,2,1,0:T(4,128)S(1)}, s32[1,1,4,512]{3,2,1,0:T(4,128)}, u32[]{:S(2)}) copy-start(s32[1,1,4,512]{3,2,1,0:T(4,128)} %param.20) | copy-start | bytes 24580
  5.8 17.0 %collective-permute-start.2 = (s32[1,2560]{1,0:T(1,128)S(1)}, s32[1,2560]{1,0:T(1,128)S(1)}, u32[]{:S(2)}, u32[]{:S(2)}) collective-permute-start(s32[1,2560]{1,0:T(1,128)S(1)} %get-tuple-element.42), channel_id=1, source_target_pairs={{0,24},{8,0},{16,8},{24,16},{1,25},{9,1},{17,9},{25,17},{2,26},{10... | collective-permute-start | bytes 30728 | tf_op jit(solution)/shard_map/ppermute | solution.py:31
  8.3 16.5 %collective-permute-start.1 = (s32[1,2560]{1,0:T(1,128)S(1)}, s32[1,2560]{1,0:T(1,128)S(1)}, u32[]{:S(2)}, u32[]{:S(2)}) collective-permute-start(s32[1,2560]{1,0:T(1,128)S(1)} %get-tuple-element.41), channel_id=1, source_target_pairs={{0,16},{8,24},{16,0},{24,8},{1,17},{9,25},{17,1},{25,9},{2,18},{10... | collective-permute-start | bytes 30728 | tf_op jit(solution)/shard_map/ppermute | solution.py:31
  8.8 19.6 %collective-permute-start = (s32[1,2560]{1,0:T(1,128)S(1)}, s32[1,2560]{1,0:T(1,128)S(1)}, u32[]{:S(2)}, u32[]{:S(2)}) collective-permute-start(s32[1,2560]{1,0:T(1,128)S(1)} %get-tuple-element.24), channel_id=1, source_target_pairs={{0,8},{8,16},{16,24},{24,0},{1,9},{9,17},{17,25},{25,1},{2,10},{10... | collective-permute-start | bytes 30728 | tf_op jit(solution)/shard_map/ppermute | solution.py:31
  10.0 11.5 %copy-start.4 = (s32[1,1,8192]{2,1,0:T(1,128)S(1)}, s32[1,1,8192]{2,1,0:T(1,128)}, u32[]{:S(2)}) copy-start(s32[1,1,8192]{2,1,0:T(1,128)} %param.22) | copy-start | bytes 98308
  14.7 14.4 %collective-permute-start.3 = (bf16[512,256]{1,0:T(8,128)(2,1)}, bf16[512,256]{1,0:T(8,128)(2,1)S(1)}, u32[]{:S(2)}, u32[]{:S(2)}) collective-permute-start(bf16[512,256]{1,0:T(8,128)(2,1)} %get-tuple-element.13), channel_id=1, source_target_pairs={{0,8},{8,16},{16,24},{1,9},{9,17},{17,25},{2,10},{10,18},{18,26},{... | collective-permute-start | bytes 786440 | tf_op jit(solution)/shard_map/ppermute | solution.py:31
  19.0 11.3 %collective-permute-start.4 = (bf16[512,256]{1,0:T(8,128)(2,1)}, bf16[512,256]{1,0:T(8,128)(2,1)S(1)}, u32[]{:S(2)}, u32[]{:S(2)}) collective-permute-start(bf16[512,256]{1,0:T(8,128)(2,1)} %get-tuple-element.14), channel_id=1, source_target_pairs={{8,0},{16,8},{24,16},{9,1},{17,9},{25,17},{10,2},{18,10},{26,18},{... | collective-permute-start | bytes 786440 | tf_op jit(solution)/shard_map/ppermute | solution.py:31
  22.8 7.9 %collective-permute-start.5 = (bf16[512,256]{1,0:T(8,128)(2,1)}, bf16[512,256]{1,0:T(8,128)(2,1)S(1)}, u32[]{:S(2)}, u32[]{:S(2)}) collective-permute-start(bf16[512,256]{1,0:T(8,128)(2,1)} %get-tuple-element.15), channel_id=1, source_target_pairs={{0,1},{1,2},{2,3},{3,4},{4,5},{5,6},{6,7},{8,9},{9,10},{10,11},{11... | collective-permute-start | bytes 786440 | tf_op jit(solution)/shard_map/ppermute | solution.py:31
  24.8 7.8 %collective-permute-start.6 = (bf16[512,256]{1,0:T(8,128)(2,1)}, bf16[512,256]{1,0:T(8,128)(2,1)S(1)}, u32[]{:S(2)}, u32[]{:S(2)}) collective-permute-start(bf16[512,256]{1,0:T(8,128)(2,1)} %get-tuple-element.16), channel_id=1, source_target_pairs={{1,0},{2,1},{3,2},{4,3},{5,4},{6,5},{7,6},{9,8},{10,9},{11,10},{12... | collective-permute-start | bytes 786440 | tf_op jit(solution)/shard_map/ppermute | solution.py:31
  29.1 3.5 %copy-start = (bf16[512,256]{1,0:T(8,128)(2,1)}, bf16[512,256]{1,0:T(8,128)(2,1)S(1)}, u32[]{:S(2)}) copy-start(bf16[512,256]{1,0:T(8,128)(2,1)S(1)} %collective-permute-done.3.h0) | copy-start | bytes 786436
  30.2 2.4 %copy-start.1 = (bf16[512,256]{1,0:T(8,128)(2,1)}, bf16[512,256]{1,0:T(8,128)(2,1)S(1)}, u32[]{:S(2)}) copy-start(bf16[512,256]{1,0:T(8,128)(2,1)S(1)} %collective-permute-done.4.h1) | copy-start | bytes 786436
  30.7 1.9 %copy-start.2 = (bf16[512,256]{1,0:T(8,128)(2,1)}, bf16[512,256]{1,0:T(8,128)(2,1)S(1)}, u32[]{:S(2)}) copy-start(bf16[512,256]{1,0:T(8,128)(2,1)S(1)} %collective-permute-done.5.h2) | copy-start | bytes 786436
  32.6 0.7 copy-start.3
  59.5 6.7 %collective-permute-start.7 = (bf16[256,256]{1,0:T(8,128)(2,1)}, bf16[256,256]{1,0:T(8,128)(2,1)S(1)}, u32[]{:S(2)}, u32[]{:S(2)}) collective-permute-start(bf16[256,256]{1,0:T(8,128)(2,1)} %get-tuple-element.19), channel_id=1, source_target_pairs={{0,8},{8,16},{16,24},{24,0},{1,9},{9,17},{17,25},{25,1},{2,10},{10... | collective-permute-start | bytes 393224 | tf_op jit(solution)/shard_map/ppermute | solution.py:31
  62.2 7.6 %collective-permute-start.8 = (bf16[256,256]{1,0:T(8,128)(2,1)}, bf16[256,256]{1,0:T(8,128)(2,1)S(1)}, u32[]{:S(2)}, u32[]{:S(2)}) collective-permute-start(bf16[256,256]{1,0:T(8,128)(2,1)} %get-tuple-element.20), channel_id=1, source_target_pairs={{0,16},{8,24},{16,0},{24,8},{1,17},{9,25},{17,1},{25,9},{2,18},{10... | collective-permute-start | bytes 393224 | tf_op jit(solution)/shard_map/ppermute | solution.py:31
  62.7 7.1 %collective-permute-start.9 = (bf16[256,256]{1,0:T(8,128)(2,1)}, bf16[256,256]{1,0:T(8,128)(2,1)S(1)}, u32[]{:S(2)}, u32[]{:S(2)}) collective-permute-start(bf16[256,256]{1,0:T(8,128)(2,1)} %get-tuple-element.21), channel_id=1, source_target_pairs={{0,24},{8,0},{16,8},{24,16},{1,25},{9,1},{17,9},{25,17},{2,26},{10... | collective-permute-start | bytes 393224 | tf_op jit(solution)/shard_map/ppermute | solution.py:31
  66.2 3.5 %copy-start.6 = (bf16[256,256]{1,0:T(8,128)(2,1)}, bf16[256,256]{1,0:T(8,128)(2,1)S(1)}, u32[]{:S(2)}) copy-start(bf16[256,256]{1,0:T(8,128)(2,1)S(1)} %collective-permute-done.7.refs_1_) | copy-start | bytes 393220
  69.7 0.6 copy-start.8
  69.7 0.7 copy-start.10
  72.3 6.7 %collective-permute-start.12 = (bf16[256,256]{1,0:T(8,128)(2,1)}, bf16[256,256]{1,0:T(8,128)(2,1)S(1)}, u32[]{:S(2)}, u32[]{:S(2)}) collective-permute-start(bf16[256,256]{1,0:T(8,128)(2,1)} %shard_map.161.refs_0_), channel_id=1, source_target_pairs={{0,24},{8,0},{16,8},{24,16},{1,25},{9,1},{17,9},{25,17},{2,26},{10... | collective-permute-start | bytes 393224 | tf_op jit(solution)/shard_map/ppermute | solution.py:31
  74.6 8.4 %collective-permute-start.11 = (bf16[256,256]{1,0:T(8,128)(2,1)}, bf16[256,256]{1,0:T(8,128)(2,1)S(1)}, u32[]{:S(2)}, u32[]{:S(2)}) collective-permute-start(bf16[256,256]{1,0:T(8,128)(2,1)} %shard_map.161.refs_0_), channel_id=1, source_target_pairs={{0,16},{8,24},{16,0},{24,8},{1,17},{9,25},{17,1},{25,9},{2,18},{10... | collective-permute-start | bytes 393224 | tf_op jit(solution)/shard_map/ppermute | solution.py:31
  76.0 6.9 %collective-permute-start.10 = (bf16[256,256]{1,0:T(8,128)(2,1)}, bf16[256,256]{1,0:T(8,128)(2,1)S(1)}, u32[]{:S(2)}, u32[]{:S(2)}) collective-permute-start(bf16[256,256]{1,0:T(8,128)(2,1)} %shard_map.161.refs_0_), channel_id=1, source_target_pairs={{0,8},{8,16},{16,24},{24,0},{1,9},{9,17},{17,25},{25,1},{2,10},{10... | collective-permute-start | bytes 393224 | tf_op jit(solution)/shard_map/ppermute | solution.py:31
  79.0 4.0 %copy-start.5 = (bf16[256,256]{1,0:T(8,128)(2,1)}, bf16[256,256]{1,0:T(8,128)(2,1)S(1)}, u32[]{:S(2)}) copy-start(bf16[256,256]{1,0:T(8,128)(2,1)S(1)} %collective-permute-done.12.refs_3_) | copy-start | bytes 393220
  82.9 0.7 copy-start.7
  83.0 0.7 copy-start.9

commit v2 on v1

v2 whole, which is shorter than its diff:
```python
import functools
import math

import jax
import jax.numpy as jnp
from jax import lax
from jax.experimental import pallas as pl
from jax.experimental.pallas import tpu as pltpu
from jax.sharding import PartitionSpec as P

F32 = jnp.float32
BF16 = jnp.bfloat16
LANES = 128
TAIL = 16
PAD = 8
FINE_CHUNK = 512
COARSE_CHUNK = 512
ROWS = 2048
LIFT = 256
VMEM_SPARE = 12 << 20

SMEM_SPEC = pl.BlockSpec(memory_space=pltpu.SMEM)
VMEM_SPEC = pl.BlockSpec(memory_space=pltpu.VMEM)
LOOSE_SPEC = pl.BlockSpec(memory_space=pltpu.VMEM)
HBM_SPEC = pl.BlockSpec(memory_space=pl.ANY)


def shifted(block, axis, distance, wrap):
    count = lax.axis_size(axis)
    route = []
    for i in range(count):
        j = i + distance
        if wrap:
            route.append((i, j % count))
        elif 0 <= j < count:
            route.append((i, j))
    return lax.ppermute(block, axis, route)


def dot(a, b):
    return jnp.dot(a, b, preferred_element_type=F32)


def silu(v):
    return (0.5 * v) * (1.0 + jnp.tanh(0.5 * v))


def put_rows(table, stride, begin, rows, values):
    table[begin : begin + rows, :] = values[:, :LANES]
    table[stride + begin : stride + begin + rows, :] = values[:, LANES:]


def project_into(table, stride, begin, states, weight):
    rows = states.shape[0]
    step = min(rows, 512)
    for at in range(0, rows, step):
        term = dot(states[at : at + step, :], weight).astype(BF16).astype(F32)
        put_rows(table, stride, begin + at, step, term)


def selection(indices, begin, rows):
    columns = indices.shape[1]
    number = lax.broadcasted_iota(jnp.int32, (rows, columns), 0) + begin
    return jnp.where(number == indices, 1.0, 0.0).astype(BF16)


def gather_rows(base, begin, end, s_ref, r_ref, ts, s_stride, tr, r_stride, buf, buf_stride):
    lines = 4
    length = (end - begin) // lines
    starts = [pl.multiple_of(base + begin + line * length, length) for line in range(lines)]
    s_of = [s_ref.at[:, pl.ds(start, length)] for start in starts]
    r_of = [r_ref.at[:, pl.ds(start, length)] for start in starts]
    for j in range(length):
        for line in range(lines):
            s = s_of[line][0, j]
            r = r_of[line][0, j]
            buf[pl.ds(begin + line * length + j, 2, stride=buf_stride), :] = (
                ts[pl.ds(s, 2, stride=s_stride), :] + tr[pl.ds(r, 2, stride=r_stride), :]
            )


def edge_sums(nodes, chunk, s_ref, r_ref, rv_ref, ts, s_stride, tr, r_stride, buf, hid, acc):
    turns = s_ref.shape[1] // chunk
    block = min(ROWS, nodes)
    stride = buf.shape[0] // 2
    acc[0:nodes, :] = jnp.zeros((nodes, 2 * LANES), F32)

    def gather(c):
        gather_rows(c * chunk, 0, chunk, s_ref, r_ref, ts, s_stride, tr, r_stride, buf, stride)

    def activate(slot):
        hid[slot, 0:chunk, :LANES] = silu(buf[0:chunk, :]).astype(BF16)
        hid[slot, 0:chunk, LANES:] = silu(buf[stride : stride + chunk, :]).astype(BF16)

    def sums(c, at):
        targets = rv_ref[:, pl.ds(pl.multiple_of(c * chunk, chunk), chunk)]
        return dot(selection(targets, at, block), hid[lax.rem(c, 2), 0:chunk, :])

    gather(0)
    activate(0)

    def turn(c, carry):
        for at in range(0, nodes - block, block):
            acc[at : at + block, :] += sums(c, at)
        added = sums(c, nodes - block)
        gather(c + 1)
        acc[nodes - block : nodes, :] += added
        activate(lax.rem(c + 1, 2))
        return carry

    if turns > 1:
        lax.fori_loop(0, turns - 1, turn, 0)
    for at in range(0, nodes, block):
        acc[at : at + block, :] += sums(turns - 1, at)


def updated(states, summed, w_ref, gain):
    aggregate = dot(summed.astype(BF16), w_ref[2]).astype(BF16)
    inner = silu(dot(states, w_ref[3]) + dot(aggregate, w_ref[4])).astype(BF16)
    output = dot(inner, w_ref[5])
    centred = output - jnp.mean(output, axis=1, keepdims=True)
    spread = jnp.mean(centred * centred, axis=1, keepdims=True)
    return states.astype(F32) + gain * centred * lax.rsqrt(spread + 1e-05)


def halo_kernel(l_ref, nodes, *refs):
    outs, (table, buf) = refs[:4], refs[4:]
    rows = nodes.shape[0]
    listed = outs[0].shape[0]
    unroll = 128
    lines = 4
    put_rows(table, rows + PAD, 0, rows, nodes[...].astype(F32))
    for d in range(4):

        def some(c, carry):
            base = pl.multiple_of(c * unroll, unroll)
            length = unroll // lines
            of = [l_ref.at[:, pl.ds(base + line * length, length)] for line in range(lines)]
            for j in range(length):
                for line in range(lines):
                    i = of[line][d, j]
                    buf[pl.ds(base + line * length + j, 2, stride=listed + PAD), :] = table[
                        pl.ds(i, 2, stride=rows + PAD), :
                    ]
            return carry

        lax.fori_loop(0, listed // unroll, some, 0)
        outs[d][:, :LANES] = buf[0:listed, :].astype(BF16)
        outs[d][:, LANES:] = buf[listed + PAD : 2 * listed + PAD, :].astype(BF16)


def count_kernel(members, p_ref, out):
    size = out.shape[1]
    eye = lax.broadcasted_iota(jnp.int32, (size, size), 0) == lax.broadcasted_iota(
        jnp.int32, (size, size), 1
    )
    parents = p_ref[...]
    line = lax.broadcasted_iota(jnp.int32, (TAIL, size), 0)
    for d in range(members):
        chosen = jnp.where(
            lax.broadcasted_iota(jnp.int32, (size, parents.shape[1]), 0) + d * size == parents,
            1.0,
            0.0,
        )
        column = jnp.sum(chosen, axis=1, keepdims=True)
        row = jnp.sum(jnp.where(eye, column, 0.0), axis=0, keepdims=True)
        upper = jnp.floor(row * (1.0 / 256.0))
        lower = row - upper * 256.0
        out[d * TAIL : (d + 1) * TAIL, :] = jnp.where(
            line == 0, lower, jnp.where(line == 1, upper, 0.0)
        ).astype(BF16)


def started(*copies):
    for copy in copies:
        copy.start()
    return copies


def fine_kernel(members, chunk, s_hbm, r_hbm, w_hbm, rv_ref, p_ref, c_ref, nodes, h0, h1, h2, h3, g_ref, *refs):
    one, parts = refs[0], refs[1 : 1 + members]
    ts, tr, buf, hid, acc, s_ref, r_ref, w_ref, sems = refs[1 + members :]
    early, late, senders, receivers = started(
        pltpu.make_async_copy(w_hbm.at[0:2], w_ref.at[0:2], sems.at[0]),
        pltpu.make_async_copy(w_hbm.at[2:6], w_ref.at[2:6], sems.at[1]),
        pltpu.make_async_copy(s_hbm, s_ref, sems.at[2]),
        pltpu.make_async_copy(r_hbm, r_ref, sems.at[3]),
    )
    count = nodes.shape[0]
    listed = h0.shape[0]
    s_stride = count + 4 * listed + PAD
    r_stride = count + PAD
    put_rows(tr, r_stride, count, PAD, jnp.zeros((PAD, 2 * LANES), F32))
    early.wait()
    project_into(ts, s_stride, 0, nodes, w_ref[0])
    for d, halo in enumerate((h0, h1, h2, h3)):
        project_into(ts, s_stride, count + d * listed, halo, w_ref[0])
    project_into(tr, r_stride, 0, nodes, w_ref[1])
    senders.wait()
    receivers.wait()
    edge_sums(count, chunk, s_ref, r_ref, rv_ref, ts, s_stride, tr, r_stride, buf, hid, acc)
    late.wait()
    gain = g_ref[0:1, :]
    step = 512
    for at in range(0, count, step):
        rows = slice(at, at + step)
        one[rows, :] = updated(nodes[rows, :], acc[rows, :], w_ref, gain).astype(BF16)
    parents = p_ref[...]
    size = parts[0].shape[0] - TAIL
    for d in range(members):
        parts[d][0:size, :] = dot(selection(parents, d * size, size), one[...]).astype(BF16)
        parts[d][size : size + TAIL, :] = c_ref[d * TAIL : (d + 1) * TAIL, :]


def mean_kernel(members, *refs):
    pieces, out = refs[:members], refs[members]
    size = out.shape[0]
    eye = lax.broadcasted_iota(jnp.int32, (size, size), 0) == lax.broadcasted_iota(
        jnp.int32, (size, size), 1
    )
    total = pieces[0][...].astype(F32)
    for piece in pieces[1:]:
        total = total + piece[...].astype(F32)
    children = total[size : size + 1, :] + 256.0 * total[size + 1 : size + 2, :]
    column = jnp.sum(jnp.where(eye, children, 0.0), axis=1, keepdims=True)
    out[...] = (total[0:size, :] / jnp.maximum(column, 1.0)).astype(BF16)


def turned(row):
    n = row.shape[1]
    return jnp.concatenate(
        [
            jnp.transpose(jnp.broadcast_to(row[:, at : at + LANES], (LANES, LANES)))
            for at in range(0, n, LANES)
        ],
        axis=0,
    )


def picks(row, columns):
    column = turned(row)
    lane = lax.broadcasted_iota(jnp.int32, column.shape, 1)
    return jnp.concatenate(
        [
            jnp.where(column == lane + at, 1.0, 0.0).astype(BF16)
            for at in range(0, columns, LANES)
        ],
        axis=1,
    )


def upper_kernel(
    members,
    chunk,
    cs_hbm,
    cr_hbm,
    ts_hbm,
    tr_hbm,
    cw_hbm,
    tw_hbm,
    crv_ref,
    trv_ref,
    tp_ref,
    p_ref,
    fine,
    g_ref,
    *refs,
):
    pieces = refs[:members]
    fine_out, coarse_out = refs[members : members + 2]
    (
        ts,
        tr,
        buf,
        hid,
        acc,
        zero,
        one,
        last,
        cs_ref,
        cr_ref,
        es_ref,
        er_ref,
        cw_ref,
        tw_ref,
        sems,
    ) = refs[members + 2 :]
    copies = started(
        pltpu.make_async_copy(cw_hbm, cw_ref, sems.at[0]),
        pltpu.make_async_copy(cs_hbm, cs_ref, sems.at[1]),
        pltpu.make_async_copy(cr_hbm, cr_ref, sems.at[2]),
        pltpu.make_async_copy(ts_hbm, es_ref, sems.at[3]),
        pltpu.make_async_copy(tr_hbm, er_ref, sems.at[4]),
        pltpu.make_async_copy(tw_hbm, tw_ref, sems.at[5]),
    )
    size = pieces[0].shape[0]
    count = size * members
    tops = count // 8
    stride = count + PAD
    for d in range(members):
        zero[d * size : (d + 1) * size, :] = pieces[d][...]
    copies[0].wait()
    project_into(ts, stride, 0, zero, cw_ref[0])
    project_into(tr, stride, 0, zero, cw_ref[1])
    for copy in copies[1:]:
        copy.wait()
    edge_sums(count, chunk, cs_ref, cr_ref, crv_ref, ts, stride, tr, stride, buf, hid, acc)
    gain = g_ref[1:2, :]
    step = min(count, 512)
    for at in range(0, count, step):
        rows = slice(at, at + step)
        one[rows, :] = updated(zero[rows, :], acc[rows, :], cw_ref, gain).astype(BF16)
    chosen = jnp.where(
        lax.broadcasted_iota(jnp.int32, (tops, count), 0) == tp_ref[...], 1.0, 0.0
    )
    held = jnp.sum(chosen, axis=1, keepdims=True)
    top_zero = (dot(chosen.astype(BF16), one[...]) / jnp.maximum(held, 1.0)).astype(BF16)
    top_stride = tops + PAD
    put_rows(ts, top_stride, 0, tops, dot(top_zero, tw_ref[0]).astype(BF16).astype(F32))
    put_rows(tr, top_stride, 0, tops, dot(top_zero, tw_ref[1]).astype(BF16).astype(F32))
    edge_sums(tops, chunk, es_ref, er_ref, trv_ref, ts, top_stride, tr, top_stride, buf, hid, acc)
    top_one = updated(top_zero, acc[0:tops, :], tw_ref, g_ref[2:3, :]).astype(BF16)
    for at in range(0, count, size):
        rows = slice(at, at + size)
        lifted = dot(picks(tp_ref[:, rows], tops), top_one)
        one[rows, :] = (one[rows, :].astype(F32) + lifted).astype(BF16)
    (done,) = started(pltpu.make_async_copy(one.at[0:size, :], coarse_out, sems.at[0]))
    leaving = [done]
    step = fine.shape[0] // 4
    for k in range(4):
        for at in range(k * step, (k + 1) * step, LIFT):
            rows = slice(at, at + LIFT)
            lifted = dot(picks(p_ref[:, rows], count), one[...])
            last[rows, :] = (fine[rows, :].astype(F32) + lifted).astype(BF16)
        rows = pl.ds(k * step, step)
        leaving += started(
            pltpu.make_async_copy(last.at[rows, :], fine_out.at[rows, :], sems.at[1 + k])
        )
    for copy in leaving:
        copy.wait()


def call(kernel, outs, out_spec, specs, scratch, *operands):
    held = sum(
        math.prod(s.shape) * s.dtype.itemsize for s in scratch if s.memory_space == pltpu.VMEM
    )
    operands = [
        pltpu.with_memory_space_constraint(x, pltpu.VMEM) if spec is VMEM_SPEC else x
        for x, spec in zip(operands, specs)
    ]
    return pl.pallas_call(
        kernel,
        out_shape=outs,
        in_specs=specs,
        out_specs=[out_spec for _ in outs],
        scratch_shapes=scratch,
        compiler_params=pltpu.CompilerParams(vmem_limit_bytes=held + VMEM_SPARE),
    )(*operands)


def body(
    fine_nodes,
    fine_weights,
    coarse_weights,
    top_weights,
    gains,
    send_list,
    fine_sender,
    fine_receiver,
    pool_owner,
    pool_local,
    coarse_sender,
    coarse_receiver,
    top_parent,
    top_sender,
    top_receiver,
):
    nodes, width = fine_nodes.shape
    members = lax.axis_size("gx")
    me = lax.axis_index("gx")
    size = nodes // 8
    count = size * members
    tops = count // 8
    listed = send_list.shape[-1]
    edges = fine_sender.shape[-1]
    shape = jax.ShapeDtypeStruct

    halo = list(
        call(
            halo_kernel,
            [shape((listed, width), BF16)] * 4,
            LOOSE_SPEC,
            [SMEM_SPEC, LOOSE_SPEC],
            [
                pltpu.VMEM((2 * (nodes + PAD), LANES), F32),
                pltpu.VMEM((2 * (listed + PAD), LANES), F32),
            ],
            send_list.reshape(4, listed),
            fine_nodes,
        )
    )
    halo[0], pool_owner, pool_local = lax.optimization_barrier((halo[0], pool_owner, pool_local))
    arrived = [
        shifted(halo[slot], axis, distance, False)
        for slot, (axis, distance) in enumerate((("gx", 1), ("gx", -1), ("gy", 1), ("gy", -1)))
    ]
    owner = pool_owner.reshape(1, -1)
    local = pool_local.reshape(1, -1)
    ahead = lax.rem(owner - me + members, members) * size + local
    behind = lax.rem(me - owner + members, members) * size + local
    (counts,) = call(
        functools.partial(count_kernel, members),
        [shape((members * TAIL, size), BF16)],
        LOOSE_SPEC,
        [LOOSE_SPEC],
        [],
        ahead,
    )
    chunk = min(FINE_CHUNK, edges)
    fine_sender = fine_sender.reshape(1, edges)
    fine_receiver = fine_receiver.reshape(1, edges)
    fine_one, *parts = call(
        functools.partial(fine_kernel, members, chunk),
        [shape((nodes, width), BF16)] + [shape((size + TAIL, width), BF16)] * members,
        LOOSE_SPEC,
        [HBM_SPEC] * 3 + [LOOSE_SPEC] * 3 + [VMEM_SPEC] * 5 + [LOOSE_SPEC],
        [
            pltpu.VMEM((2 * (nodes + 4 * listed + PAD), LANES), F32),
            pltpu.VMEM((2 * (nodes + PAD), LANES), F32),
            pltpu.VMEM((2 * (chunk + PAD), LANES), F32),
            pltpu.VMEM((2, chunk, width), BF16),
            pltpu.VMEM((nodes, width), F32),
            pltpu.SMEM((1, edges), jnp.int32),
            pltpu.SMEM((1, edges), jnp.int32),
            pltpu.VMEM(fine_weights.shape, BF16),
            pltpu.SemaphoreType.DMA((4,)),
        ],
        fine_sender,
        fine_receiver,
        fine_weights,
        fine_receiver,
        ahead,
        counts,
        fine_nodes,
        *arrived,
        gains,
    )
    parts = [parts[0]] + [shifted(parts[d], "gx", d, True) for d in range(1, members)]
    if members > 1:
        parts[1], coarse_sender, coarse_receiver, top_parent = lax.optimization_barrier(
            (parts[1], coarse_sender, coarse_receiver, top_parent)
        )
    share = jnp.concatenate(
        [coarse_sender.reshape(1, -1), coarse_receiver.reshape(1, -1), top_parent.reshape(1, -1)],
        axis=1,
    )
    mixed = [share] + [shifted(share, "gx", d, True) for d in range(1, members)]
    per = coarse_sender.shape[-1]
    senders = jnp.concatenate([piece[:, :per] for piece in mixed], axis=1)
    senders = lax.rem(me - senders // size + members, members) * size + lax.rem(senders, size)
    receivers = jnp.concatenate(
        [piece[:, per : 2 * per] + d * size for d, piece in enumerate(mixed)], axis=1
    )
    tops_of = jnp.concatenate([piece[:, 2 * per :] for piece in mixed], axis=1)

    (zero,) = call(
        functools.partial(mean_kernel, members),
        [shape((size, width), BF16)],
        LOOSE_SPEC,
        [LOOSE_SPEC] + [VMEM_SPEC] * (members - 1),
        [],
        *parts,
    )
    zeros = [zero] + [shifted(zero, "gx", d, True) for d in range(1, members)]

    top_edges = top_sender.shape[-1]
    chunk = min(COARSE_CHUNK, per * members, top_edges)
    fine_state, coarse_state = call(
        functools.partial(upper_kernel, members, chunk),
        [shape((nodes, width), BF16), shape((size, width), BF16)],
        HBM_SPEC,
        [HBM_SPEC] * 6 + [LOOSE_SPEC] * 4 + [VMEM_SPEC] + [LOOSE_SPEC] * 2 + [VMEM_SPEC] * (members - 1),
        [
            pltpu.VMEM((2 * (count + PAD), LANES), F32),
            pltpu.VMEM((2 * (count + PAD), LANES), F32),
            pltpu.VMEM((2 * (chunk + PAD), LANES), F32),
            pltpu.VMEM((2, chunk, width), BF16),
            pltpu.VMEM((count, width), F32),
            pltpu.VMEM((count, width), BF16),
            pltpu.VMEM((count, width), BF16),
            pltpu.VMEM((nodes, width), BF16),
            pltpu.SMEM((1, per * members), jnp.int32),
            pltpu.SMEM((1, per * members), jnp.int32),
            pltpu.SMEM((1, top_edges), jnp.int32),
            pltpu.SMEM((1, top_edges), jnp.int32),
            pltpu.VMEM(coarse_weights.shape, BF16),
            pltpu.VMEM(top_weights.shape, BF16),
            pltpu.SemaphoreType.DMA((6,)),
        ],
        senders,
        receivers,
        top_sender,
        top_receiver,
        coarse_weights,
        top_weights,
        receivers,
        top_receiver,
        tops_of,
        behind,
        fine_one,
        gains,
        *zeros,
    )
    return (fine_state, coarse_state[None])


def solution(mesh):
    placed = (
        P(("gx", "gy"), None),
        P(),
        P(),
        P(),
        P(),
        P("gx", "gy", None, None),
        P("gx", "gy", None),
        P("gx", "gy", None),
        P(("gx", "gy"), None),
        P(("gx", "gy")),
        P("gy", "gx"),
        P("gy", "gx"),
        P("gy", "gx"),
        P("gy", None),
        P("gy", None),
    )
    return jax.shard_map(
        body,
        mesh=mesh,
        in_specs=placed,
        out_specs=(P(("gx", "gy"), None), P("gy", "gx", None)),
        check_vma=False,
    )
```

time: 99.9 us -> 84.3 us (0.84)
  the two profiles are of different devices: /device:TPU:16 before, /device:TPU:0 now
where the time goes in v2:
time: 84.3 us; the launch traced here: 83.8 us
  Pallas kernels  41.4 us (49%)
  starting transfers between devices  17.9 us (21%)
  waiting for transfers between devices  17.8 us (21%)
  local copies, waits for them, and re-layouts  5.56 us (7%)
  between operations  1.07 us (1%)
    pallas_call x5, Pallas kernels, call(): pl.pallas_call(kernel, out_shape=outs, in_specs=specs, out_specs=[out_spe...  41.4 us
    ppermute x13, starting transfers between devices, shifted(): return lax.ppermute(block, axis, route)  17.9 us
    ppermute x13, waiting for transfers between devices, shifted(): return lax.ppermute(block, axis, route)  17.8 us
    unnamed x38, local copies, waits for them, and re-layouts  4.86 us
  transfers between devices with their start and end apart: 13, of which 5 were waited for; matrix products, arithmetic and copies ran while one was open for 0% of the time, Pallas kernels for 1%

profile of v2, /device:TPU:0, one launch (start us, length us, event | category | flops | bytes accessed | tf_op | source)
XLA Modules:
  0.0 83.8 jit_solution(11545632021635264940)
XLA Ops:
  0.6 1.2 %copy-done = bf16[2048,256]{1,0:T(8,128)(2,1)S(1)} copy-done((bf16[2048,256]{1,0:T(8,128)(2,1)S(1)}, bf16[2048,256]{1,0:T(8,128)(2,1)}, u32[]{:S(2)}) %copy-start) | copy-done | bytes 1048600
  1.9 0.7 copy-done.8
  2.6 2.9 %shard_map.158 = (bf16[512,256]{1,0:T(8,128)(2,1)S(1)}, bf16[512,256]{1,0:T(8,128)(2,1)S(1)}, bf16[512,256]{1,0:T(8,128)(2,1)S(1)}, bf16[512,256]{1,0:T(8,128)(2,1)S(1)}) custom-call(s32[4,512]{1,0:T(4,128)S(1)} %bitcast.14, bf16[2048,256]{1,0:T(8,128)(2,1)S(1)} %copy-done), custom_call_target="tpu_custom_call" | custom-call | tf_op jit(solution)/shard_map/pallas_call | solution.py:351
  5.4 4.9 %collective-permute-start = (bf16[512,256]{1,0:T(8,128)(2,1)S(1)}, bf16[512,256]{1,0:T(8,128)(2,1)S(1)}, u32[]{:S(2)}, u32[]{:S(2)}) collective-permute-start(bf16[512,256]{1,0:T(8,128)(2,1)S(1)} %get-tuple-element.23), channel_id=1, source_target_pairs={{0,8},{8,16},{16,24},{1,9},{9,17},{17,25},{2,10},{10,18},{18,26},{... | collective-permute-start | bytes 786440 | tf_op jit(solution)/shard_map/ppermute | solution.py:37
  10.3 1.3 %collective-permute-start.1 = (bf16[512,256]{1,0:T(8,128)(2,1)S(1)}, bf16[512,256]{1,0:T(8,128)(2,1)S(1)}, u32[]{:S(2)}, u32[]{:S(2)}) collective-permute-start(bf16[512,256]{1,0:T(8,128)(2,1)S(1)} %get-tuple-element.24), channel_id=1, source_target_pairs={{8,0},{16,8},{24,16},{9,1},{17,9},{25,17},{10,2},{18,10},{26,18},{... | collective-permute-start | bytes 786440 | tf_op jit(solution)/shard_map/ppermute | solution.py:37
  11.6 1.5 %collective-permute-start.2 = (bf16[512,256]{1,0:T(8,128)(2,1)S(1)}, bf16[512,256]{1,0:T(8,128)(2,1)S(1)}, u32[]{:S(2)}, u32[]{:S(2)}) collective-permute-start(bf16[512,256]{1,0:T(8,128)(2,1)S(1)} %get-tuple-element.25), channel_id=1, source_target_pairs={{0,1},{1,2},{2,3},{3,4},{4,5},{5,6},{6,7},{8,9},{9,10},{10,11},{11... | collective-permute-start | bytes 786440 | tf_op jit(solution)/shard_map/ppermute | solution.py:37
  13.1 1.3 %collective-permute-start.3 = (bf16[512,256]{1,0:T(8,128)(2,1)S(1)}, bf16[512,256]{1,0:T(8,128)(2,1)S(1)}, u32[]{:S(2)}, u32[]{:S(2)}) collective-permute-start(bf16[512,256]{1,0:T(8,128)(2,1)S(1)} %get-tuple-element.26), channel_id=1, source_target_pairs={{1,0},{2,1},{3,2},{4,3},{5,4},{6,5},{7,6},{9,8},{10,9},{11,10},{12... | collective-permute-start | bytes 786440 | tf_op jit(solution)/shard_map/ppermute | solution.py:37
  14.5 0.7 copy-done.16
  15.2 1.0 %shard_map.159.c_ref = bf16[64,256]{1,0:T(8,128)(2,1)S(1)} custom-call(s32[1,2048]{1,0:T(1,128)S(1)} %bitcast.10), custom_call_target="tpu_custom_call" | custom-call | tf_op jit(solution)/shard_map/pallas_call | solution.py:351
  16.1 7.3 %collective-permute-done.1.h1 = bf16[512,256]{1,0:T(8,128)(2,1)S(1)} collective-permute-done((bf16[512,256]{1,0:T(8,128)(2,1)S(1)}, bf16[512,256]{1,0:T(8,128)(2,1)S(1)}, u32[]{:S(2)}, u32[]{:S(2)}) %collective-permute-start.1) | collective-permute-done | bytes 262176 | tf_op jit(solution)/shard_map/ppermute | solution.py:37
  23.5 1.1 %copy-done.2 = bf16[6,256,256]{2,1,0:T(8,128)(2,1)S(1)} copy-done((bf16[6,256,256]{2,1,0:T(8,128)(2,1)S(1)}, bf16[6,256,256]{2,1,0:T(8,128)(2,1)}, u32[]{:S(2)}) %copy-start.2) | copy-done | bytes 786456
  24.6 22.9 %shard_map.160 = (bf16[2048,256]{1,0:T(8,128)(2,1)S(1)}, bf16[272,256]{1,0:T(8,128)(2,1)S(1)}, bf16[272,256]{1,0:T(8,128)(2,1)S(1)}, bf16[272,256]{1,0:T(8,128)(2,1)S(1)}, bf16[272,256]{1,0:T(8,128)(2,1)S(1)}) custom-call(s32[1,8192]{1,0:T(1,128)S(1)} %bitcast.12, s32[1,8192]{1,0:T(1,128)S(1)} %bitcast.8, bf16[6,256,256]{2,1,0:T(8,128)(2,1)S(1)} %copy-done.2, ...), custom_call_target="tpu_custom_call" | custom-call | tf_op jit(solution)/shard_map/pallas_call | solution.py:351
  47.5 1.5 %collective-permute-start.4 = (bf16[272,256]{1,0:T(8,128)(2,1)S(1)}, bf16[272,256]{1,0:T(8,128)(2,1)S(1)}, u32[]{:S(2)}, u32[]{:S(2)}) collective-permute-start(bf16[272,256]{1,0:T(8,128)(2,1)S(1)} %get-tuple-element.27), channel_id=1, source_target_pairs={{0,8},{8,16},{16,24},{24,0},{1,9},{9,17},{17,25},{25,1},{2,10},{10... | collective-permute-start | bytes 417800 | tf_op jit(solution)/shard_map/ppermute | solution.py:37
  49.0 1.5 %collective-permute-start.9 = (bf16[272,256]{1,0:T(8,128)(2,1)S(1)}, bf16[272,256]{1,0:T(8,128)(2,1)S(1)}, u32[]{:S(2)}, u32[]{:S(2)}) collective-permute-start(bf16[272,256]{1,0:T(8,128)(2,1)S(1)} %get-tuple-element.35), channel_id=1, source_target_pairs={{0,24},{8,0},{16,8},{24,16},{1,25},{9,1},{17,9},{25,17},{2,26},{10... | collective-permute-start | bytes 417800 | tf_op jit(solution)/shard_map/ppermute | solution.py:37
  50.5 4.5 %collective-permute-done.4.refs_1_ = bf16[272,256]{1,0:T(8,128)(2,1)S(1)} collective-permute-done((bf16[272,256]{1,0:T(8,128)(2,1)S(1)}, bf16[272,256]{1,0:T(8,128)(2,1)S(1)}, u32[]{:S(2)}, u32[]{:S(2)}) %collective-permute-start.4) | collective-permute-done | bytes 139296 | tf_op jit(solution)/shard_map/ppermute | solution.py:37
  55.1 0.1 collective-permute-start.7
  55.2 1.6 %collective-permute-start.6 = (s32[1,2304]{1,0:T(1,128)S(1)}, s32[1,2304]{1,0:T(1,128)S(1)}, u32[]{:S(2)}, u32[]{:S(2)}) collective-permute-start(s32[1,2304]{1,0:T(1,128)S(1)} %constant_dynamic-update-slice_fusion), channel_id=1, source_target_pairs={{0,16},{8,24},{16,0},{24,8},{1,17},{9,25},{17,1},{25,9},{2,18},{10... | collective-permute-start | bytes 27656 | tf_op jit(solution)/shard_map/ppermute | solution.py:37
  56.8 0.4 collective-permute-start.5
  57.2 0.3 collective-permute-done.8.refs_2_
  57.4 0.1 shard_map.161.refs_0_
  57.6 2.8 %collective-permute-start.12 = (bf16[256,256]{1,0:T(8,128)(2,1)S(1)}, bf16[256,256]{1,0:T(8,128)(2,1)S(1)}, u32[]{:S(2)}, u32[]{:S(2)}) collective-permute-start(bf16[256,256]{1,0:T(8,128)(2,1)S(1)} %shard_map.161.refs_0_), channel_id=1, source_target_pairs={{0,24},{8,0},{16,8},{24,16},{1,25},{9,1},{17,9},{25,17},{2,26},{10... | collective-permute-start | bytes 393224 | tf_op jit(solution)/shard_map/ppermute | solution.py:37
  60.4 1.0 %collective-permute-start.10 = (bf16[256,256]{1,0:T(8,128)(2,1)S(1)}, bf16[256,256]{1,0:T(8,128)(2,1)S(1)}, u32[]{:S(2)}, u32[]{:S(2)}) collective-permute-start(bf16[256,256]{1,0:T(8,128)(2,1)S(1)} %shard_map.161.refs_0_), channel_id=1, source_target_pairs={{0,8},{8,16},{16,24},{24,0},{1,9},{9,17},{17,25},{25,1},{2,10},{10... | collective-permute-start | bytes 393224 | tf_op jit(solution)/shard_map/ppermute | solution.py:37
  61.4 0.0 copy-start.14
  61.5 0.1 fusion.2
  61.6 0.4 copy-done.14
  62.0 0.7 slice-done
  62.7 0.0 slice-done.1
  62.7 1.6 %collective-permute-done.12.refs_3_ = bf16[256,256]{1,0:T(8,128)(2,1)S(1)} collective-permute-done((bf16[256,256]{1,0:T(8,128)(2,1)S(1)}, bf16[256,256]{1,0:T(8,128)(2,1)S(1)}, u32[]{:S(2)}, u32[]{:S(2)}) %collective-permute-start.12) | collective-permute-done | bytes 131104 | tf_op jit(solution)/shard_map/ppermute | solution.py:37
  64.3 4.1 %collective-permute-done.11.refs_2_ = bf16[256,256]{1,0:T(8,128)(2,1)S(1)} collective-permute-done((bf16[256,256]{1,0:T(8,128)(2,1)S(1)}, bf16[256,256]{1,0:T(8,128)(2,1)S(1)}, u32[]{:S(2)}, u32[]{:S(2)}) %collective-permute-start.11) | collective-permute-done | bytes 131104 | tf_op jit(solution)/shard_map/ppermute | solution.py:37
  68.4 0.7 copy-done.10
  69.1 0.0 copy-done.9
  69.1 14.5 %shard_map.162 = (bf16[2048,256]{1,0:T(8,128)(2,1)}, bf16[256,256]{1,0:T(8,128)(2,1)}) custom-call(s32[1,4096]{1,0:T(1,128)S(1)} %get-tuple-element.48.cs_hbm, s32[1,4096]{1,0:T(1,128)S(1)} %get-tuple-element.49.cr_hbm.crv_ref, s32[1,512]{1,0:T(1,128)S(1)} %copy-done.10, s32[1,512]{1,0:T(1,128)S(1)} %copy-done.9, bf16[6,256,256]{2,1,0:T(8,128)(2,1)S(1)} %copy-done.3, ...), custom_call_target="tpu_custom_call" | custom-call | tf_op jit(solution)/shard_map/pallas_call | solution.py:351
  (50 shorter events, 0.2 us)
Async XLA Ops:
  0.6 1.2 %copy-start = (bf16[2048,256]{1,0:T(8,128)(2,1)S(1)}, bf16[2048,256]{1,0:T(8,128)(2,1)}, u32[]{:S(2)}) copy-start(bf16[2048,256]{1,0:T(8,128)(2,1)} %nodes.3) | copy-start | bytes 3145732
  1.9 0.7 copy-start.8
  2.6 20.9 %copy-start.1 = (bf16[2048,256]{1,0:T(8,128)(2,1)S(1)}, bf16[2048,256]{1,0:T(8,128)(2,1)}, u32[]{:S(2)}) copy-start(bf16[2048,256]{1,0:T(8,128)(2,1)} %nodes.3) | copy-start | bytes 3145732
  5.4 9.0 %copy-start.15 = (s32[2048,1]{0,1:T(1,128)S(1)}, s32[2048,1]{0,1:T(1,128)}, u32[]{:S(2)}) copy-start(s32[2048,1]{0,1:T(1,128)} %param.23) | copy-start | bytes 24580
  5.4 10.7 %collective-permute-start = (bf16[512,256]{1,0:T(8,128)(2,1)S(1)}, bf16[512,256]{1,0:T(8,128)(2,1)S(1)}, u32[]{:S(2)}, u32[]{:S(2)}) collective-permute-start(bf16[512,256]{1,0:T(8,128)(2,1)S(1)} %get-tuple-element.23), channel_id=1, source_target_pairs={{0,8},{8,16},{16,24},{1,9},{9,17},{17,25},{2,10},{10,18},{18,26},{... | collective-permute-start | bytes 786440 | tf_op jit(solution)/shard_map/ppermute | solution.py:37
  10.3 13.1 %collective-permute-start.1 = (bf16[512,256]{1,0:T(8,128)(2,1)S(1)}, bf16[512,256]{1,0:T(8,128)(2,1)S(1)}, u32[]{:S(2)}, u32[]{:S(2)}) collective-permute-start(bf16[512,256]{1,0:T(8,128)(2,1)S(1)} %get-tuple-element.24), channel_id=1, source_target_pairs={{8,0},{16,8},{24,16},{9,1},{17,9},{25,17},{10,2},{18,10},{26,18},{... | collective-permute-start | bytes 786440 | tf_op jit(solution)/shard_map/ppermute | solution.py:37
  11.6 11.8 %collective-permute-start.2 = (bf16[512,256]{1,0:T(8,128)(2,1)S(1)}, bf16[512,256]{1,0:T(8,128)(2,1)S(1)}, u32[]{:S(2)}, u32[]{:S(2)}) collective-permute-start(bf16[512,256]{1,0:T(8,128)(2,1)S(1)} %get-tuple-element.25), channel_id=1, source_target_pairs={{0,1},{1,2},{2,3},{3,4},{4,5},{5,6},{6,7},{8,9},{9,10},{10,11},{11... | collective-permute-start | bytes 786440 | tf_op jit(solution)/shard_map/ppermute | solution.py:37
  13.1 10.3 %collective-permute-start.3 = (bf16[512,256]{1,0:T(8,128)(2,1)S(1)}, bf16[512,256]{1,0:T(8,128)(2,1)S(1)}, u32[]{:S(2)}, u32[]{:S(2)}) collective-permute-start(bf16[512,256]{1,0:T(8,128)(2,1)S(1)} %get-tuple-element.26), channel_id=1, source_target_pairs={{1,0},{2,1},{3,2},{4,3},{5,4},{6,5},{7,6},{9,8},{10,9},{11,10},{12... | collective-permute-start | bytes 786440 | tf_op jit(solution)/shard_map/ppermute | solution.py:37
  14.4 0.7 copy-start.16
  15.1 8.3 %copy-start.6 = (s32[1,1,8192]{2,1,0:T(1,128)S(1)}, s32[1,1,8192]{2,1,0:T(1,128)}, u32[]{:S(2)}) copy-start(s32[1,1,8192]{2,1,0:T(1,128)} %param.21) | copy-start | bytes 98308
  15.1 8.3 %copy-start.5 = (s32[1,1,8192]{2,1,0:T(1,128)S(1)}, s32[1,1,8192]{2,1,0:T(1,128)}, u32[]{:S(2)}) copy-start(s32[1,1,8192]{2,1,0:T(1,128)} %param.22) | copy-start | bytes 98308
  15.2 8.3 %copy-start.7 = (f32[3,256]{1,0:T(4,128)S(1)}, f32[3,256]{1,0:T(4,128)}, u32[]{:S(2)}) copy-start(f32[3,256]{1,0:T(4,128)} %g_ref.3) | copy-start | bytes 9220
  23.5 1.1 %copy-start.2 = (bf16[6,256,256]{2,1,0:T(8,128)(2,1)S(1)}, bf16[6,256,256]{2,1,0:T(8,128)(2,1)}, u32[]{:S(2)}) copy-start(bf16[6,256,256]{2,1,0:T(8,128)(2,1)} %w_hbm.1) | copy-start | bytes 2359300
  24.6 30.4 %copy-start.11 = (s32[1,1024]{1,0:T(1,128)S(1)}, s32[1,1024]{1,0:T(1,128)}, u32[]{:S(2)}) copy-start(s32[1,1024]{1,0:T(1,128)} %param.25) | copy-start | bytes 12292
  24.6 30.5 %copy-start.12 = (s32[1,1024]{1,0:T(1,128)S(1)}, s32[1,1024]{1,0:T(1,128)}, u32[]{:S(2)}) copy-start(s32[1,1024]{1,0:T(1,128)} %param.26) | copy-start | bytes 12292
  24.6 30.5 %copy-start.17 = (s32[1,256]{1,0:T(1,128)S(1)}, s32[1,256]{1,0:T(1,128)}, u32[]{:S(2)}) copy-start(s32[1,256]{1,0:T(1,128)} %param.27) | copy-start | bytes 3076
  24.6 43.8 %copy-start.4 = (bf16[6,256,256]{2,1,0:T(8,128)(2,1)S(1)}, bf16[6,256,256]{2,1,0:T(8,128)(2,1)}, u32[]{:S(2)}) copy-start(bf16[6,256,256]{2,1,0:T(8,128)(2,1)} %tw_hbm.1) | copy-start | bytes 2359300
  47.5 20.9 %copy-start.3 = (bf16[6,256,256]{2,1,0:T(8,128)(2,1)S(1)}, bf16[6,256,256]{2,1,0:T(8,128)(2,1)}, u32[]{:S(2)}) copy-start(bf16[6,256,256]{2,1,0:T(8,128)(2,1)} %cw_hbm.1) | copy-start | bytes 2359300
  47.5 7.5 %collective-permute-start.4 = (bf16[272,256]{1,0:T(8,128)(2,1)S(1)}, bf16[272,256]{1,0:T(8,128)(2,1)S(1)}, u32[]{:S(2)}, u32[]{:S(2)}) collective-permute-start(bf16[272,256]{1,0:T(8,128)(2,1)S(1)} %get-tuple-element.27), channel_id=1, source_target_pairs={{0,8},{8,16},{16,24},{24,0},{1,9},{9,17},{17,25},{25,1},{2,10},{10... | collective-permute-start | bytes 417800 | tf_op jit(solution)/shard_map/ppermute | solution.py:37
  49.0 8.4 %collective-permute-start.8 = (bf16[272,256]{1,0:T(8,128)(2,1)S(1)}, bf16[272,256]{1,0:T(8,128)(2,1)S(1)}, u32[]{:S(2)}, u32[]{:S(2)}) collective-permute-start(bf16[272,256]{1,0:T(8,128)(2,1)S(1)} %get-tuple-element.34), channel_id=1, source_target_pairs={{0,16},{8,24},{16,0},{24,8},{1,17},{9,25},{17,1},{25,9},{2,18},{10... | collective-permute-start | bytes 417800 | tf_op jit(solution)/shard_map/ppermute | solution.py:37
  49.0 8.4 %collective-permute-start.9 = (bf16[272,256]{1,0:T(8,128)(2,1)S(1)}, bf16[272,256]{1,0:T(8,128)(2,1)S(1)}, u32[]{:S(2)}, u32[]{:S(2)}) collective-permute-start(bf16[272,256]{1,0:T(8,128)(2,1)S(1)} %get-tuple-element.35), channel_id=1, source_target_pairs={{0,24},{8,0},{16,8},{24,16},{1,25},{9,1},{17,9},{25,17},{2,26},{10... | collective-permute-start | bytes 417800 | tf_op jit(solution)/shard_map/ppermute | solution.py:37
  55.1 5.3 %collective-permute-start.7 = (s32[1,2304]{1,0:T(1,128)S(1)}, s32[1,2304]{1,0:T(1,128)S(1)}, u32[]{:S(2)}, u32[]{:S(2)}) collective-permute-start(s32[1,2304]{1,0:T(1,128)S(1)} %constant_dynamic-update-slice_fusion), channel_id=1, source_target_pairs={{0,24},{8,0},{16,8},{24,16},{1,25},{9,1},{17,9},{25,17},{2,26},{10... | collective-permute-start | bytes 27656 | tf_op jit(solution)/shard_map/ppermute | solution.py:37
  55.2 6.3 %collective-permute-start.6 = (s32[1,2304]{1,0:T(1,128)S(1)}, s32[1,2304]{1,0:T(1,128)S(1)}, u32[]{:S(2)}, u32[]{:S(2)}) collective-permute-start(s32[1,2304]{1,0:T(1,128)S(1)} %constant_dynamic-update-slice_fusion), channel_id=1, source_target_pairs={{0,16},{8,24},{16,0},{24,8},{1,17},{9,25},{17,1},{25,9},{2,18},{10... | collective-permute-start | bytes 27656 | tf_op jit(solution)/shard_map/ppermute | solution.py:37
  56.8 4.7 %collective-permute-start.5 = (s32[1,2304]{1,0:T(1,128)S(1)}, s32[1,2304]{1,0:T(1,128)S(1)}, u32[]{:S(2)}, u32[]{:S(2)}) collective-permute-start(s32[1,2304]{1,0:T(1,128)S(1)} %constant_dynamic-update-slice_fusion), channel_id=1, source_target_pairs={{0,8},{8,16},{16,24},{24,0},{1,9},{9,17},{17,25},{25,1},{2,10},{10... | collective-permute-start | bytes 27656 | tf_op jit(solution)/shard_map/ppermute | solution.py:37
  57.6 6.8 %collective-permute-start.12 = (bf16[256,256]{1,0:T(8,128)(2,1)S(1)}, bf16[256,256]{1,0:T(8,128)(2,1)S(1)}, u32[]{:S(2)}, u32[]{:S(2)}) collective-permute-start(bf16[256,256]{1,0:T(8,128)(2,1)S(1)} %shard_map.161.refs_0_), channel_id=1, source_target_pairs={{0,24},{8,0},{16,8},{24,16},{1,25},{9,1},{17,9},{25,17},{2,26},{10... | collective-permute-start | bytes 393224 | tf_op jit(solution)/shard_map/ppermute | solution.py:37
  60.4 8.0 %collective-permute-start.11 = (bf16[256,256]{1,0:T(8,128)(2,1)S(1)}, bf16[256,256]{1,0:T(8,128)(2,1)S(1)}, u32[]{:S(2)}, u32[]{:S(2)}) collective-permute-start(bf16[256,256]{1,0:T(8,128)(2,1)S(1)} %shard_map.161.refs_0_), channel_id=1, source_target_pairs={{0,16},{8,24},{16,0},{24,8},{1,17},{9,25},{17,1},{25,9},{2,18},{10... | collective-permute-start | bytes 393224 | tf_op jit(solution)/shard_map/ppermute | solution.py:37
  60.4 1.2 %copy-start.13 = (s32[1,2304]{1,0:T(1,128)}, s32[1,2304]{1,0:T(1,128)S(1)}, u32[]{:S(2)}) copy-start(s32[1,2304]{1,0:T(1,128)S(1)} %collective-permute-done.7) | copy-start | bytes 27652
  60.4 8.0 %collective-permute-start.10 = (bf16[256,256]{1,0:T(8,128)(2,1)S(1)}, bf16[256,256]{1,0:T(8,128)(2,1)S(1)}, u32[]{:S(2)}, u32[]{:S(2)}) collective-permute-start(bf16[256,256]{1,0:T(8,128)(2,1)S(1)} %shard_map.161.refs_0_), channel_id=1, source_target_pairs={{0,8},{8,16},{16,24},{24,0},{1,9},{9,17},{17,25},{25,1},{2,10},{10... | collective-permute-start | bytes 393224 | tf_op jit(solution)/shard_map/ppermute | solution.py:37
  62.0 0.7 slice-start
  62.0 0.7 slice-start.1
  68.4 0.7 copy-start.10
  68.4 0.7 copy-start.9
  (1 other events, 0.6 us)

commit v3 on v2

--- a/solution.py
+++ b/solution.py
@@ -13,7 +13,7 @@
 LANES = 128
 TAIL = 16
 PAD = 8
-FINE_CHUNK = 512
+FINE_CHUNK = 1024
 COARSE_CHUNK = 512
 ROWS = 2048
 LIFT = 256
@@ -149,7 +149,18 @@
         outs[d][:, LANES:] = buf[listed + PAD : 2 * listed + PAD, :].astype(BF16)
 
 
-def count_kernel(members, p_ref, out):
+def started(*copies):
+    for copy in copies:
+        copy.start()
+    return copies
+
+
+def count_kernel(members, p_ref, w_hbm, s_hbm, r_hbm, out, w_out, s_out, r_out, sems):
+    copies = started(
+        pltpu.make_async_copy(w_hbm, w_out, sems.at[0]),
+        pltpu.make_async_copy(s_hbm, s_out, sems.at[1]),
+        pltpu.make_async_copy(r_hbm, r_out, sems.at[2]),
+    )
     size = out.shape[1]
     eye = lax.broadcasted_iota(jnp.int32, (size, size), 0) == lax.broadcasted_iota(
         jnp.int32, (size, size), 1
@@ -169,29 +180,22 @@
         out[d * TAIL : (d + 1) * TAIL, :] = jnp.where(
             line == 0, lower, jnp.where(line == 1, upper, 0.0)
         ).astype(BF16)
-
-
-def started(*copies):
     for copy in copies:
-        copy.start()
-    return copies
-
-
-def fine_kernel(members, chunk, s_hbm, r_hbm, w_hbm, rv_ref, p_ref, c_ref, nodes, h0, h1, h2, h3, g_ref, *refs):
+        copy.wait()
+
+
+def fine_kernel(members, chunk, s_hbm, r_hbm, w_ref, rv_ref, p_ref, c_ref, nodes, h0, h1, h2, h3, g_ref, *refs):
     one, parts = refs[0], refs[1 : 1 + members]
-    ts, tr, buf, hid, acc, s_ref, r_ref, w_ref, sems = refs[1 + members :]
-    early, late, senders, receivers = started(
-        pltpu.make_async_copy(w_hbm.at[0:2], w_ref.at[0:2], sems.at[0]),
-        pltpu.make_async_copy(w_hbm.at[2:6], w_ref.at[2:6], sems.at[1]),
-        pltpu.make_async_copy(s_hbm, s_ref, sems.at[2]),
-        pltpu.make_async_copy(r_hbm, r_ref, sems.at[3]),
+    ts, tr, buf, hid, acc, s_ref, r_ref, sems = refs[1 + members :]
+    senders, receivers = started(
+        pltpu.make_async_copy(s_hbm, s_ref, sems.at[0]),
+        pltpu.make_async_copy(r_hbm, r_ref, sems.at[1]),
     )
     count = nodes.shape[0]
     listed = h0.shape[0]
     s_stride = count + 4 * listed + PAD
     r_stride = count + PAD
     put_rows(tr, r_stride, count, PAD, jnp.zeros((PAD, 2 * LANES), F32))
-    early.wait()
     project_into(ts, s_stride, 0, nodes, w_ref[0])
     for d, halo in enumerate((h0, h1, h2, h3)):
         project_into(ts, s_stride, count + d * listed, halo, w_ref[0])
@@ -199,7 +203,6 @@
     senders.wait()
     receivers.wait()
     edge_sums(count, chunk, s_ref, r_ref, rv_ref, ts, s_stride, tr, r_stride, buf, hid, acc)
-    late.wait()
     gain = g_ref[0:1, :]
     step = 512
     for at in range(0, count, step):
@@ -342,7 +345,7 @@
 
 def call(kernel, outs, out_spec, specs, scratch, *operands):
     held = sum(
-        math.prod(s.shape) * s.dtype.itemsize for s in scratch if s.memory_space == pltpu.VMEM
+        math.prod(s.shape) * s.dtype.itemsize for s in scratch if getattr(s, "memory_space", None) == pltpu.VMEM
     )
     operands = [
         pltpu.with_memory_space_constraint(x, pltpu.VMEM) if spec is VMEM_SPEC else x
@@ -408,13 +411,22 @@
     local = pool_local.reshape(1, -1)
     ahead = lax.rem(owner - me + members, members) * size + local
     behind = lax.rem(me - owner + members, members) * size + local
-    (counts,) = call(
+    top_edges = top_sender.shape[-1]
+    counts, fine_weights, top_sender, top_receiver = call(
         functools.partial(count_kernel, members),
-        [shape((members * TAIL, size), BF16)],
+        [
+            shape((members * TAIL, size), BF16),
+            shape(fine_weights.shape, BF16),
+            shape((1, top_edges), jnp.int32),
+            shape((1, top_edges), jnp.int32),
+        ],
         LOOSE_SPEC,
-        [LOOSE_SPEC],
-        [],
+        [LOOSE_SPEC] + [HBM_SPEC] * 3,
+        [pltpu.SemaphoreType.DMA((3,))],
         ahead,
+        fine_weights,
+        top_sender,
+        top_receiver,
     )
     chunk = min(FINE_CHUNK, edges)
     fine_sender = fine_sender.reshape(1, edges)
@@ -423,7 +435,7 @@
         functools.partial(fine_kernel, members, chunk),
         [shape((nodes, width), BF16)] + [shape((size + TAIL, width), BF16)] * members,
         LOOSE_SPEC,
-        [HBM_SPEC] * 3 + [LOOSE_SPEC] * 3 + [VMEM_SPEC] * 5 + [LOOSE_SPEC],
+        [HBM_SPEC] * 2 + [VMEM_SPEC] + [LOOSE_SPEC] * 3 + [VMEM_SPEC] * 5 + [LOOSE_SPEC],
         [
             pltpu.VMEM((2 * (nodes + 4 * listed + PAD), LANES), F32),
             pltpu.VMEM((2 * (nodes + PAD), LANES), F32),
@@ -432,8 +444,7 @@
             pltpu.VMEM((nodes, width), F32),
             pltpu.SMEM((1, edges), jnp.int32),
             pltpu.SMEM((1, edges), jnp.int32),
-            pltpu.VMEM(fine_weights.shape, BF16),
-            pltpu.SemaphoreType.DMA((4,)),
+            pltpu.SemaphoreType.DMA((2,)),
         ],
         fine_sender,
         fine_receiver,
@@ -473,7 +484,6 @@
     )
     zeros = [zero] + [shifted(zero, "gx", d, True) for d in range(1, members)]
 
-    top_edges = top_sender.shape[-1]
     chunk = min(COARSE_CHUNK, per * members, top_edges)
     fine_state, coarse_state = call(
         functools.partial(upper_kernel, members, chunk),

time: 84.3 us -> 82.7 us (0.981)
  waiting for transfers between devices: 17.8 us -> 15.9 us
    ppermute x13, waiting for transfers between devices: 17.8 us -> 15.9 us  [shifted(): return lax.ppermute(block, axis, route)]
where the time goes in v3:
time: 82.7 us; the launch traced here: 82.2 us
  Pallas kernels  41.4 us (50%)
  starting transfers between devices  18.2 us (22%)
  waiting for transfers between devices  15.9 us (19%)
  local copies, waits for them, and re-layouts  5.56 us (7%)
  between operations  1.07 us (1%)
    pallas_call x5, Pallas kernels, call(): pl.pallas_call(kernel, out_shape=outs, in_specs=specs, out_specs=[out_spe...  41.4 us
    ppermute x13, starting transfers between devices, shifted(): return lax.ppermute(block, axis, route)  18.2 us
    ppermute x13, waiting for transfers between devices, shifted(): return lax.ppermute(block, axis, route)  15.9 us
    unnamed x38, local copies, waits for them, and re-layouts  4.86 us
  transfers between devices with their start and end apart: 13, of which 5 were waited for; matrix products, arithmetic and copies ran while one was open for 0% of the time, Pallas kernels for 1%

profile of v3, /device:TPU:0, one launch (start us, length us, event | category | flops | bytes accessed | tf_op | source)
XLA Modules:
  0.0 82.2 jit_solution(695354576677842885)
XLA Ops:
  0.6 1.2 %copy-done = bf16[2048,256]{1,0:T(8,128)(2,1)S(1)} copy-done((bf16[2048,256]{1,0:T(8,128)(2,1)S(1)}, bf16[2048,256]{1,0:T(8,128)(2,1)}, u32[]{:S(2)}) %copy-start) | copy-done | bytes 1048600
  1.9 0.7 copy-done.8
  2.6 2.9 %shard_map.158 = (bf16[512,256]{1,0:T(8,128)(2,1)S(1)}, bf16[512,256]{1,0:T(8,128)(2,1)S(1)}, bf16[512,256]{1,0:T(8,128)(2,1)S(1)}, bf16[512,256]{1,0:T(8,128)(2,1)S(1)}) custom-call(s32[4,512]{1,0:T(4,128)S(1)} %bitcast.14, bf16[2048,256]{1,0:T(8,128)(2,1)S(1)} %copy-done), custom_call_target="tpu_custom_call" | custom-call | tf_op jit(solution)/shard_map/pallas_call | solution.py:354
  5.4 4.9 %collective-permute-start = (bf16[512,256]{1,0:T(8,128)(2,1)S(1)}, bf16[512,256]{1,0:T(8,128)(2,1)S(1)}, u32[]{:S(2)}, u32[]{:S(2)}) collective-permute-start(bf16[512,256]{1,0:T(8,128)(2,1)S(1)} %get-tuple-element.29), channel_id=1, source_target_pairs={{0,8},{8,16},{16,24},{1,9},{9,17},{17,25},{2,10},{10,18},{18,26},{... | collective-permute-start | bytes 786440 | tf_op jit(solution)/shard_map/ppermute | solution.py:37
  10.3 1.3 %collective-permute-start.1 = (bf16[512,256]{1,0:T(8,128)(2,1)S(1)}, bf16[512,256]{1,0:T(8,128)(2,1)S(1)}, u32[]{:S(2)}, u32[]{:S(2)}) collective-permute-start(bf16[512,256]{1,0:T(8,128)(2,1)S(1)} %get-tuple-element.30), channel_id=1, source_target_pairs={{8,0},{16,8},{24,16},{9,1},{17,9},{25,17},{10,2},{18,10},{26,18},{... | collective-permute-start | bytes 786440 | tf_op jit(solution)/shard_map/ppermute | solution.py:37
  11.6 1.5 %collective-permute-start.2 = (bf16[512,256]{1,0:T(8,128)(2,1)S(1)}, bf16[512,256]{1,0:T(8,128)(2,1)S(1)}, u32[]{:S(2)}, u32[]{:S(2)}) collective-permute-start(bf16[512,256]{1,0:T(8,128)(2,1)S(1)} %get-tuple-element.31), channel_id=1, source_target_pairs={{0,1},{1,2},{2,3},{3,4},{4,5},{5,6},{6,7},{8,9},{9,10},{10,11},{11... | collective-permute-start | bytes 786440 | tf_op jit(solution)/shard_map/ppermute | solution.py:37
  13.1 1.3 %collective-permute-start.3 = (bf16[512,256]{1,0:T(8,128)(2,1)S(1)}, bf16[512,256]{1,0:T(8,128)(2,1)S(1)}, u32[]{:S(2)}, u32[]{:S(2)}) collective-permute-start(bf16[512,256]{1,0:T(8,128)(2,1)S(1)} %get-tuple-element.32), channel_id=1, source_target_pairs={{1,0},{2,1},{3,2},{4,3},{5,4},{6,5},{7,6},{9,8},{10,9},{11,10},{12... | collective-permute-start | bytes 786440 | tf_op jit(solution)/shard_map/ppermute | solution.py:37
  14.5 0.7 copy-done.16
  15.2 0.7 copy-done.10
  15.8 0.0 copy-done.9
  15.8 1.1 %copy-done.2 = bf16[6,256,256]{2,1,0:T(8,128)(2,1)S(1)} copy-done((bf16[6,256,256]{2,1,0:T(8,128)(2,1)S(1)}, bf16[6,256,256]{2,1,0:T(8,128)(2,1)}, u32[]{:S(2)}) %copy-start.2) | copy-done | bytes 786456
  17.0 1.0 %shard_map.159 = (bf16[64,256]{1,0:T(8,128)(2,1)S(1)}, bf16[6,256,256]{2,1,0:T(8,128)(2,1)S(1)}, s32[1,512]{1,0:T(1,128)S(1)}, s32[1,512]{1,0:T(1,128)S(1)}) custom-call(s32[1,2048]{1,0:T(1,128)S(1)} %bitcast.10, bf16[6,256,256]{2,1,0:T(8,128)(2,1)S(1)} %copy-done.2, s32[1,512]{1,0:T(1,128)S(1)} %copy-done.9, s32[1,512]{1,0:T(1,128)S(1)} %copy-done.10), custom_call_target="tpu_custom_call" | custom-call | tf_op jit(solution)/shard_map/pallas_call | solution.py:354
  18.0 5.4 %collective-permute-done.1.h1 = bf16[512,256]{1,0:T(8,128)(2,1)S(1)} collective-permute-done((bf16[512,256]{1,0:T(8,128)(2,1)S(1)}, bf16[512,256]{1,0:T(8,128)(2,1)S(1)}, u32[]{:S(2)}, u32[]{:S(2)}) %collective-permute-start.1) | collective-permute-done | bytes 262176 | tf_op jit(solution)/shard_map/ppermute | solution.py:37
  23.5 22.8 %shard_map.160 = (bf16[2048,256]{1,0:T(8,128)(2,1)S(1)}, bf16[272,256]{1,0:T(8,128)(2,1)S(1)}, bf16[272,256]{1,0:T(8,128)(2,1)S(1)}, bf16[272,256]{1,0:T(8,128)(2,1)S(1)}, bf16[272,256]{1,0:T(8,128)(2,1)S(1)}) custom-call(s32[1,8192]{1,0:T(1,128)S(1)} %bitcast.12, s32[1,8192]{1,0:T(1,128)S(1)} %bitcast.8, bf16[6,256,256]{2,1,0:T(8,128)(2,1)S(1)} %get-tuple-element.27.w_ref, ...), custom_call_target="tpu_custom_call" | custom-call | tf_op jit(solution)/shard_map/pallas_call | solution.py:354
  46.3 1.8 %collective-permute-start.4 = (bf16[272,256]{1,0:T(8,128)(2,1)S(1)}, bf16[272,256]{1,0:T(8,128)(2,1)S(1)}, u32[]{:S(2)}, u32[]{:S(2)}) collective-permute-start(bf16[272,256]{1,0:T(8,128)(2,1)S(1)} %get-tuple-element.33), channel_id=1, source_target_pairs={{0,8},{8,16},{16,24},{24,0},{1,9},{9,17},{17,25},{25,1},{2,10},{10... | collective-permute-start | bytes 417800 | tf_op jit(solution)/shard_map/ppermute | solution.py:37
  48.2 1.5 %collective-permute-start.9 = (bf16[272,256]{1,0:T(8,128)(2,1)S(1)}, bf16[272,256]{1,0:T(8,128)(2,1)S(1)}, u32[]{:S(2)}, u32[]{:S(2)}) collective-permute-start(bf16[272,256]{1,0:T(8,128)(2,1)S(1)} %get-tuple-element.43), channel_id=1, source_target_pairs={{0,24},{8,0},{16,8},{24,16},{1,25},{9,1},{17,9},{25,17},{2,26},{10... | collective-permute-start | bytes 417800 | tf_op jit(solution)/shard_map/ppermute | solution.py:37
  49.7 4.3 %collective-permute-done.4.refs_1_ = bf16[272,256]{1,0:T(8,128)(2,1)S(1)} collective-permute-done((bf16[272,256]{1,0:T(8,128)(2,1)S(1)}, bf16[272,256]{1,0:T(8,128)(2,1)S(1)}, u32[]{:S(2)}, u32[]{:S(2)}) %collective-permute-start.4) | collective-permute-done | bytes 139296 | tf_op jit(solution)/shard_map/ppermute | solution.py:37
  54.1 0.1 collective-permute-start.7
  54.2 1.7 %collective-permute-start.6 = (s32[1,2304]{1,0:T(1,128)S(1)}, s32[1,2304]{1,0:T(1,128)S(1)}, u32[]{:S(2)}, u32[]{:S(2)}) collective-permute-start(s32[1,2304]{1,0:T(1,128)S(1)} %constant_dynamic-update-slice_fusion), channel_id=1, source_target_pairs={{0,16},{8,24},{16,0},{24,8},{1,17},{9,25},{17,1},{25,9},{2,18},{10... | collective-permute-start | bytes 27656 | tf_op jit(solution)/shard_map/ppermute | solution.py:37
  55.9 0.3 collective-permute-start.5
  56.2 0.3 collective-permute-done.8.refs_2_
  56.5 0.1 shard_map.161.refs_0_
  56.6 2.6 %collective-permute-start.12 = (bf16[256,256]{1,0:T(8,128)(2,1)S(1)}, bf16[256,256]{1,0:T(8,128)(2,1)S(1)}, u32[]{:S(2)}, u32[]{:S(2)}) collective-permute-start(bf16[256,256]{1,0:T(8,128)(2,1)S(1)} %shard_map.161.refs_0_), channel_id=1, source_target_pairs={{0,24},{8,0},{16,8},{24,16},{1,25},{9,1},{17,9},{25,17},{2,26},{10... | collective-permute-start | bytes 393224 | tf_op jit(solution)/shard_map/ppermute | solution.py:37
  59.3 0.1 collective-permute-start.11
  59.4 1.0 %collective-permute-start.10 = (bf16[256,256]{1,0:T(8,128)(2,1)S(1)}, bf16[256,256]{1,0:T(8,128)(2,1)S(1)}, u32[]{:S(2)}, u32[]{:S(2)}) collective-permute-start(bf16[256,256]{1,0:T(8,128)(2,1)S(1)} %shard_map.161.refs_0_), channel_id=1, source_target_pairs={{0,8},{8,16},{16,24},{24,0},{1,9},{9,17},{17,25},{25,1},{2,10},{10... | collective-permute-start | bytes 393224 | tf_op jit(solution)/shard_map/ppermute | solution.py:37
  60.5 0.0 collective-permute-done.5
  60.5 0.1 fusion.2
  60.6 0.4 copy-done.14
  61.0 0.7 slice-done
  61.7 1.5 %collective-permute-done.12.refs_3_ = bf16[256,256]{1,0:T(8,128)(2,1)S(1)} collective-permute-done((bf16[256,256]{1,0:T(8,128)(2,1)S(1)}, bf16[256,256]{1,0:T(8,128)(2,1)S(1)}, u32[]{:S(2)}, u32[]{:S(2)}) %collective-permute-start.12) | collective-permute-done | bytes 131104 | tf_op jit(solution)/shard_map/ppermute | solution.py:37
  63.2 4.3 %collective-permute-done.11.refs_2_ = bf16[256,256]{1,0:T(8,128)(2,1)S(1)} collective-permute-done((bf16[256,256]{1,0:T(8,128)(2,1)S(1)}, bf16[256,256]{1,0:T(8,128)(2,1)S(1)}, u32[]{:S(2)}, u32[]{:S(2)}) %collective-permute-start.11) | collective-permute-done | bytes 131104 | tf_op jit(solution)/shard_map/ppermute | solution.py:37
  67.5 14.6 %shard_map.162 = (bf16[2048,256]{1,0:T(8,128)(2,1)}, bf16[256,256]{1,0:T(8,128)(2,1)}) custom-call(s32[1,4096]{1,0:T(1,128)S(1)} %get-tuple-element.56.cs_hbm, s32[1,4096]{1,0:T(1,128)S(1)} %get-tuple-element.57.cr_hbm.crv_ref, s32[1,512]{1,0:T(1,128)S(1)} %get-tuple-element.37.ts_hbm, s32[1,512]{1,0:T(1,128)S(1)} %get-tuple-element.38.tr_hbm.trv_ref, ...), custom_call_target="tpu_custom_call" | custom-call | tf_op jit(solution)/shard_map/pallas_call | solution.py:354
  (50 shorter events, 0.2 us)
Async XLA Ops:
  0.6 1.2 %copy-start = (bf16[2048,256]{1,0:T(8,128)(2,1)S(1)}, bf16[2048,256]{1,0:T(8,128)(2,1)}, u32[]{:S(2)}) copy-start(bf16[2048,256]{1,0:T(8,128)(2,1)} %nodes.3) | copy-start | bytes 3145732
  1.9 0.7 copy-start.8
  2.6 20.9 %copy-start.1 = (bf16[2048,256]{1,0:T(8,128)(2,1)S(1)}, bf16[2048,256]{1,0:T(8,128)(2,1)}, u32[]{:S(2)}) copy-start(bf16[2048,256]{1,0:T(8,128)(2,1)} %nodes.3) | copy-start | bytes 3145732
  5.4 9.0 %copy-start.15 = (s32[2048,1]{0,1:T(1,128)S(1)}, s32[2048,1]{0,1:T(1,128)}, u32[]{:S(2)}) copy-start(s32[2048,1]{0,1:T(1,128)} %param.23) | copy-start | bytes 24580
  5.4 12.6 %collective-permute-start = (bf16[512,256]{1,0:T(8,128)(2,1)S(1)}, bf16[512,256]{1,0:T(8,128)(2,1)S(1)}, u32[]{:S(2)}, u32[]{:S(2)}) collective-permute-start(bf16[512,256]{1,0:T(8,128)(2,1)S(1)} %get-tuple-element.29), channel_id=1, source_target_pairs={{0,8},{8,16},{16,24},{1,9},{9,17},{17,25},{2,10},{10,18},{18,26},{... | collective-permute-start | bytes 786440 | tf_op jit(solution)/shard_map/ppermute | solution.py:37
  10.3 13.1 %collective-permute-start.1 = (bf16[512,256]{1,0:T(8,128)(2,1)S(1)}, bf16[512,256]{1,0:T(8,128)(2,1)S(1)}, u32[]{:S(2)}, u32[]{:S(2)}) collective-permute-start(bf16[512,256]{1,0:T(8,128)(2,1)S(1)} %get-tuple-element.30), channel_id=1, source_target_pairs={{8,0},{16,8},{24,16},{9,1},{17,9},{25,17},{10,2},{18,10},{26,18},{... | collective-permute-start | bytes 786440 | tf_op jit(solution)/shard_map/ppermute | solution.py:37
  11.6 11.8 %collective-permute-start.2 = (bf16[512,256]{1,0:T(8,128)(2,1)S(1)}, bf16[512,256]{1,0:T(8,128)(2,1)S(1)}, u32[]{:S(2)}, u32[]{:S(2)}) collective-permute-start(bf16[512,256]{1,0:T(8,128)(2,1)S(1)} %get-tuple-element.31), channel_id=1, source_target_pairs={{0,1},{1,2},{2,3},{3,4},{4,5},{5,6},{6,7},{8,9},{9,10},{10,11},{11... | collective-permute-start | bytes 786440 | tf_op jit(solution)/shard_map/ppermute | solution.py:37
  13.1 10.3 %collective-permute-start.3 = (bf16[512,256]{1,0:T(8,128)(2,1)S(1)}, bf16[512,256]{1,0:T(8,128)(2,1)S(1)}, u32[]{:S(2)}, u32[]{:S(2)}) collective-permute-start(bf16[512,256]{1,0:T(8,128)(2,1)S(1)} %get-tuple-element.32), channel_id=1, source_target_pairs={{1,0},{2,1},{3,2},{4,3},{5,4},{6,5},{7,6},{9,8},{10,9},{11,10},{12... | collective-permute-start | bytes 786440 | tf_op jit(solution)/shard_map/ppermute | solution.py:37
  14.4 0.7 copy-start.16
  15.1 0.7 copy-start.10
  15.1 0.7 copy-start.9
  15.8 1.1 %copy-start.2 = (bf16[6,256,256]{2,1,0:T(8,128)(2,1)S(1)}, bf16[6,256,256]{2,1,0:T(8,128)(2,1)}, u32[]{:S(2)}) copy-start(bf16[6,256,256]{2,1,0:T(8,128)(2,1)} %w_hbm.1) | copy-start | bytes 2359300
  17.0 6.5 %copy-start.5 = (s32[1,1,8192]{2,1,0:T(1,128)S(1)}, s32[1,1,8192]{2,1,0:T(1,128)}, u32[]{:S(2)}) copy-start(s32[1,1,8192]{2,1,0:T(1,128)} %param.22) | copy-start | bytes 98308
  17.0 6.5 %copy-start.6 = (s32[1,1,8192]{2,1,0:T(1,128)S(1)}, s32[1,1,8192]{2,1,0:T(1,128)}, u32[]{:S(2)}) copy-start(s32[1,1,8192]{2,1,0:T(1,128)} %param.21) | copy-start | bytes 98308
  18.0 5.4 %copy-start.7 = (f32[3,256]{1,0:T(4,128)S(1)}, f32[3,256]{1,0:T(4,128)}, u32[]{:S(2)}) copy-start(f32[3,256]{1,0:T(4,128)} %g_ref.3) | copy-start | bytes 9220
  23.5 30.6 %copy-start.11 = (s32[1,1024]{1,0:T(1,128)S(1)}, s32[1,1024]{1,0:T(1,128)}, u32[]{:S(2)}) copy-start(s32[1,1024]{1,0:T(1,128)} %param.25) | copy-start | bytes 12292
  23.5 30.6 %copy-start.12 = (s32[1,1024]{1,0:T(1,128)S(1)}, s32[1,1024]{1,0:T(1,128)}, u32[]{:S(2)}) copy-start(s32[1,1024]{1,0:T(1,128)} %param.26) | copy-start | bytes 12292
  23.5 30.6 %copy-start.17 = (s32[1,256]{1,0:T(1,128)S(1)}, s32[1,256]{1,0:T(1,128)}, u32[]{:S(2)}) copy-start(s32[1,256]{1,0:T(1,128)} %param.27) | copy-start | bytes 3076
  23.5 44.0 %copy-start.4 = (bf16[6,256,256]{2,1,0:T(8,128)(2,1)S(1)}, bf16[6,256,256]{2,1,0:T(8,128)(2,1)}, u32[]{:S(2)}) copy-start(bf16[6,256,256]{2,1,0:T(8,128)(2,1)} %tw_hbm.1) | copy-start | bytes 2359300
  46.3 21.2 %copy-start.3 = (bf16[6,256,256]{2,1,0:T(8,128)(2,1)S(1)}, bf16[6,256,256]{2,1,0:T(8,128)(2,1)}, u32[]{:S(2)}) copy-start(bf16[6,256,256]{2,1,0:T(8,128)(2,1)} %cw_hbm.1) | copy-start | bytes 2359300
  46.3 7.7 %collective-permute-start.4 = (bf16[272,256]{1,0:T(8,128)(2,1)S(1)}, bf16[272,256]{1,0:T(8,128)(2,1)S(1)}, u32[]{:S(2)}, u32[]{:S(2)}) collective-permute-start(bf16[272,256]{1,0:T(8,128)(2,1)S(1)} %get-tuple-element.33), channel_id=1, source_target_pairs={{0,8},{8,16},{16,24},{24,0},{1,9},{9,17},{17,25},{25,1},{2,10},{10... | collective-permute-start | bytes 417800 | tf_op jit(solution)/shard_map/ppermute | solution.py:37
  48.2 8.3 %collective-permute-start.8 = (bf16[272,256]{1,0:T(8,128)(2,1)S(1)}, bf16[272,256]{1,0:T(8,128)(2,1)S(1)}, u32[]{:S(2)}, u32[]{:S(2)}) collective-permute-start(bf16[272,256]{1,0:T(8,128)(2,1)S(1)} %get-tuple-element.42), channel_id=1, source_target_pairs={{0,16},{8,24},{16,0},{24,8},{1,17},{9,25},{17,1},{25,9},{2,18},{10... | collective-permute-start | bytes 417800 | tf_op jit(solution)/shard_map/ppermute | solution.py:37
  48.2 8.3 %collective-permute-start.9 = (bf16[272,256]{1,0:T(8,128)(2,1)S(1)}, bf16[272,256]{1,0:T(8,128)(2,1)S(1)}, u32[]{:S(2)}, u32[]{:S(2)}) collective-permute-start(bf16[272,256]{1,0:T(8,128)(2,1)S(1)} %get-tuple-element.43), channel_id=1, source_target_pairs={{0,24},{8,0},{16,8},{24,16},{1,25},{9,1},{17,9},{25,17},{2,26},{10... | collective-permute-start | bytes 417800 | tf_op jit(solution)/shard_map/ppermute | solution.py:37
  54.1 5.3 %collective-permute-start.7 = (s32[1,2304]{1,0:T(1,128)S(1)}, s32[1,2304]{1,0:T(1,128)S(1)}, u32[]{:S(2)}, u32[]{:S(2)}) collective-permute-start(s32[1,2304]{1,0:T(1,128)S(1)} %constant_dynamic-update-slice_fusion), channel_id=1, source_target_pairs={{0,24},{8,0},{16,8},{24,16},{1,25},{9,1},{17,9},{25,17},{2,26},{10... | collective-permute-start | bytes 27656 | tf_op jit(solution)/shard_map/ppermute | solution.py:37
  54.2 6.3 %collective-permute-start.6 = (s32[1,2304]{1,0:T(1,128)S(1)}, s32[1,2304]{1,0:T(1,128)S(1)}, u32[]{:S(2)}, u32[]{:S(2)}) collective-permute-start(s32[1,2304]{1,0:T(1,128)S(1)} %constant_dynamic-update-slice_fusion), channel_id=1, source_target_pairs={{0,16},{8,24},{16,0},{24,8},{1,17},{9,25},{17,1},{25,9},{2,18},{10... | collective-permute-start | bytes 27656 | tf_op jit(solution)/shard_map/ppermute | solution.py:37
  55.9 4.6 %collective-permute-start.5 = (s32[1,2304]{1,0:T(1,128)S(1)}, s32[1,2304]{1,0:T(1,128)S(1)}, u32[]{:S(2)}, u32[]{:S(2)}) collective-permute-start(s32[1,2304]{1,0:T(1,128)S(1)} %constant_dynamic-update-slice_fusion), channel_id=1, source_target_pairs={{0,8},{8,16},{16,24},{24,0},{1,9},{9,17},{17,25},{25,1},{2,10},{10... | collective-permute-start | bytes 27656 | tf_op jit(solution)/shard_map/ppermute | solution.py:37
  56.6 6.6 %collective-permute-start.12 = (bf16[256,256]{1,0:T(8,128)(2,1)S(1)}, bf16[256,256]{1,0:T(8,128)(2,1)S(1)}, u32[]{:S(2)}, u32[]{:S(2)}) collective-permute-start(bf16[256,256]{1,0:T(8,128)(2,1)S(1)} %shard_map.161.refs_0_), channel_id=1, source_target_pairs={{0,24},{8,0},{16,8},{24,16},{1,25},{9,1},{17,9},{25,17},{2,26},{10... | collective-permute-start | bytes 393224 | tf_op jit(solution)/shard_map/ppermute | solution.py:37
  59.3 8.2 %collective-permute-start.11 = (bf16[256,256]{1,0:T(8,128)(2,1)S(1)}, bf16[256,256]{1,0:T(8,128)(2,1)S(1)}, u32[]{:S(2)}, u32[]{:S(2)}) collective-permute-start(bf16[256,256]{1,0:T(8,128)(2,1)S(1)} %shard_map.161.refs_0_), channel_id=1, source_target_pairs={{0,16},{8,24},{16,0},{24,8},{1,17},{9,25},{17,1},{25,9},{2,18},{10... | collective-permute-start | bytes 393224 | tf_op jit(solution)/shard_map/ppermute | solution.py:37
  59.4 1.3 %copy-start.13 = (s32[1,2304]{1,0:T(1,128)}, s32[1,2304]{1,0:T(1,128)S(1)}, u32[]{:S(2)}) copy-start(s32[1,2304]{1,0:T(1,128)S(1)} %collective-permute-done.7) | copy-start | bytes 27652
  59.4 8.1 %collective-permute-start.10 = (bf16[256,256]{1,0:T(8,128)(2,1)S(1)}, bf16[256,256]{1,0:T(8,128)(2,1)S(1)}, u32[]{:S(2)}, u32[]{:S(2)}) collective-permute-start(bf16[256,256]{1,0:T(8,128)(2,1)S(1)} %shard_map.161.refs_0_), channel_id=1, source_target_pairs={{0,8},{8,16},{16,24},{24,0},{1,9},{9,17},{17,25},{25,1},{2,10},{10... | collective-permute-start | bytes 393224 | tf_op jit(solution)/shard_map/ppermute | solution.py:37
  61.0 0.7 slice-start
  61.0 0.7 slice-start.1
  (1 other events, 0.6 us)
